TPU v7x, 32 devices: a whole 2x2x4 slice. The times are simulated.
32 devices in a mesh: grp: 2 (over y), ep: 4 (over z), tp: 2 (over x), mb: 2 (over core).
Axes of the slice: x: 2, y: 2, z: 4, core: 2. Of those that a mesh axis runs over, the one named last changes fastest.
Arguments:
- hidden: bfloat16 [256, 3584], P(('grp', 'ep', 'mb'), 'tp'), parts along dimension 0, may hold values from -12 to 12
- moe_gain: float32 [3584], P('tp'), may hold values from 0.1 to 1.9
- expert_ids: int32 [256, 8], P(('grp', 'ep', 'mb')), parts along dimension 0, may hold values from 0 to 7, as said below
- slots: int32 [256, 8], P(('grp', 'ep', 'mb')), parts along dimension 0, may hold values from 0 to 15, as said below
- affinity: float32 [256, 8], P(('grp', 'ep', 'mb')), parts along dimension 0, may hold values from 0.05 to 1
- w_gate: bfloat16 [8, 3584, 1024], P(('ep', 'mb'), None, 'tp'), may hold values from -0.09375 to 0.09375
- w_up: bfloat16 [8, 3584, 1024], P(('ep', 'mb'), None, 'tp'), may hold values from -0.09375 to 0.09375
- w_down: bfloat16 [8, 1024, 3584], P(('ep', 'mb'), 'tp'), may hold values from -0.1875 to 0.1875
- attn_gain: float32 [3584], P('tp'), may hold values from 0.1 to 1.9
- w_dkv: bfloat16 [3584, 576], P('tp'), may hold values from -0.09375 to 0.09375
- kv_gain: float32 [512], replicated, may hold values from 0.1 to 1.9
- queries: bfloat16 [256, 64, 576], P(('grp', 'ep', 'mb'), 'tp'), parts along dimension 0, may hold values from -36 to 36
- cache: bfloat16 [256, 128, 576], P(('grp', 'ep', 'mb'), 'tp'), parts along dimension 0, may hold values from -4 to 4
- lengths: int32 [256], P(('grp', 'ep', 'mb')), parts along dimension 0, may hold values from 2 to 128
Outputs:
- next_hidden: bfloat16 [256, 3584], P(('grp', 'ep', 'mb'), 'tp'), parts along dimension 0
- latent_out: bfloat16 [256, 64, 512], P(('grp', 'ep', 'mb'), 'tp'), parts along dimension 0
There are 2 independent parts, one for each index of `grp`. A program takes and returns all parts, laid end to end along the dimension named above; an argument that names none is the same for every part. Nothing has to cross between parts.
Inputs may be any that keep to these rules, and one draw needn't show every extreme that they name: `expert_ids`: each row names 8 different experts; in every draw some expert is named by every token. slots[t, k] is the rank of the choice (t, k) among the choices of the same expert made by the 16 tokens of one device; these ranks are distinct and run from 0 upward. A choice whose slot is 8 or more is dropped.
All inputs are finite; a program needn't handle non-finite values.
Results may differ from a plain program's by a relative error of at most 0.017.
Values may be sent and summed in bfloat16 or wider, within the bound.
A program may use at most 128 MiB of HBM per device.

v0:
```python
import functools

import jax
import jax.numpy as jnp
from jax import lax
from jax.experimental import pallas as pl
from jax.experimental.pallas import tpu as pltpu
from jax.sharding import PartitionSpec as P

CAP = 8
GROUPS = 4
epsilon = 1e-06
route_scale = 2.5
score_scale = 192.0 ** (-0.5)
MESH = pl.DeviceIdType.MESH
F32 = jnp.float32
BF16 = jnp.bfloat16


def up(value, step):
    return -(-value // step) * step


def kernel(
    n_tp,
    n_ep,
    n_mb,
    hidden,
    moe_gain,
    ids,
    slots,
    affinity,
    w_gate,
    w_up,
    w_down,
    attn_gain,
    w_dkv,
    kv_gain,
    queries,
    cache,
    lengths,
    next_out,
    latent_out,
    hid_all,
    gain_all,
    send,
    arrived,
    wg,
    wu,
    wd,
    wk,
    ret_send,
    ret,
    tsum,
    rs_send,
    rs_recv,
    key_send,
    key_recv,
    q_buf,
    kv_buf,
    acc,
    peaks,
    masses,
    keys,
    load_sem,
    kv_load_sem,
    hid_ssem,
    hid_rsem,
    gain_ssem,
    gain_rsem,
    kv_ssem,
    kv_rsem,
    row_ssem,
    row_rsem,
    ret_ssem,
    ret_rsem,
    rs_ssem,
    rs_rsem,
    key_ssem,
    key_rsem,
):
    experts = n_ep * n_mb
    tokens, d_loc = hidden.shape
    d_all = d_loc * n_tp
    lat = kv_gain.shape[1]
    kvc = cache.shape[2]
    per_group = tokens // GROUPS
    tp = lax.axis_index("tp")
    me = lax.axis_index("ep") * n_mb + lax.axis_index("mb")

    def tp_id(step):
        return lax.rem(tp + step, n_tp)

    def ex_id(step):
        return lax.rem(me + step, experts)

    def ex_dev(index):
        return {"ep": index // n_mb, "mb": lax.rem(index, n_mb)}

    local = [
        pltpu.make_async_copy(hidden, hid_all.at[tp], load_sem.at[0]),
        pltpu.make_async_copy(queries, q_buf, load_sem.at[1]),
        pltpu.make_async_copy(w_gate.at[0], wg, load_sem.at[2]),
        pltpu.make_async_copy(w_up.at[0], wu, load_sem.at[3]),
        pltpu.make_async_copy(w_down.at[0], wd, load_sem.at[4]),
        pltpu.make_async_copy(w_dkv, wk, load_sem.at[5]),
    ]
    kv_load = pltpu.make_async_copy(cache, kv_buf.at[:, tp], kv_load_sem)
    local[0].start()
    gain_all[tp] = moe_gain[...].reshape(1, d_loc)

    barrier = pltpu.get_barrier_semaphore()
    for step in range(1, n_tp):
        pl.semaphore_signal(barrier, inc=1, device_id={"tp": tp_id(step)}, device_id_type=MESH)
    for step in range(1, experts):
        pl.semaphore_signal(barrier, inc=1, device_id=ex_dev(ex_id(step)), device_id_type=MESH)
    kept = slots[...] < CAP
    aff = affinity[...]
    weight = route_scale * aff / jnp.sum(aff, 0, keepdims=True) * kept.astype(F32)
    target = jnp.where(kept, ids[...] * CAP + slots[...], -1)
    rows = experts * CAP
    iota = lax.broadcasted_iota(jnp.int32, (rows, tokens), 0)
    dispatch = jnp.zeros((rows, tokens), F32)
    combine = jnp.zeros((rows, tokens), F32)
    for k in range(ids.shape[0]):
        match = target[k : k + 1] == iota
        dispatch = jnp.where(match, 1.0, dispatch)
        combine = jnp.where(match, weight[k : k + 1], combine)
    dispatch = dispatch.astype(BF16)
    combine = combine.T
    high = combine.astype(BF16)
    rest = combine - high.astype(F32)
    mid = rest.astype(BF16)
    low = (rest - mid.astype(F32)).astype(BF16)
    combine3 = jnp.concatenate([high, mid, low], 0)

    def pick(block):
        picked = jnp.dot(dispatch, hid_all[block], preferred_element_type=F32)
        send[:, block] = picked.reshape(experts, CAP, d_loc).astype(BF16)

    def ship(block, turn):
        for step in range(1, experts):
            peer = ex_id(step)
            copy = pltpu.make_async_remote_copy(
                src_ref=send.at[peer, block],
                dst_ref=arrived.at[me, block],
                send_sem=row_ssem.at[step, turn],
                recv_sem=row_rsem.at[me, block],
                device_id=ex_dev(peer),
                device_id_type=MESH,
            )
            copy.start()
            sends.append(copy)
        arrived[me, block] = send[me, block]

    local[0].wait()
    pick(tp)
    pl.semaphore_wait(barrier, n_tp - 1 + experts - 1)

    def tp_copy(src, dst, ssem, rsem, step):
        return pltpu.make_async_remote_copy(
            src_ref=src,
            dst_ref=dst,
            send_sem=ssem,
            recv_sem=rsem,
            device_id={"tp": tp_id(step)},
            device_id_type=MESH,
        )

    def arrival(dst, rsem):
        return pltpu.make_async_copy(dst, dst, rsem)

    sends = []
    for step in range(1, n_tp):
        for src, dst, ssem, rsem in (
            (hidden, hid_all, hid_ssem, hid_rsem),
            (gain_all.at[tp], gain_all, gain_ssem, gain_rsem),
        ):
            copy = tp_copy(src, dst.at[tp], ssem.at[step], rsem.at[tp], step)
            copy.start()
            sends.append(copy)
    ship(tp, 0)
    for g in range(GROUPS):
        span = pl.ds(g * per_group, per_group)
        for step in range(1, n_tp):
            copy = tp_copy(
                cache.at[span], kv_buf.at[span, tp], kv_ssem.at[step, g], kv_rsem.at[tp, g], step
            )
            copy.start()
            sends.append(copy)
    for copy in local[1:4]:
        copy.start()
    kv_load.start()
    for copy in local[4:]:
        copy.start()

    for step in range(1, n_tp):
        arrival(hid_all.at[tp_id(step)], hid_rsem.at[tp_id(step)]).wait()
        arrival(gain_all.at[tp_id(step)], gain_rsem.at[tp_id(step)]).wait()
    for turn in range(1, n_tp):
        pick(tp_id(turn))
        ship(tp_id(turn), turn)

    local[1].wait()
    kv_load.wait()
    heads = queries.shape[1]
    span_len = cache.shape[1]
    total_len = n_tp * span_len

    def attend(g):
        span = pl.ds(g * per_group, per_group)
        for step in range(1, n_tp):
            arrival(kv_buf.at[span, tp_id(step)], kv_rsem.at[tp_id(step), g]).wait()

        def body(i, carry):
            t = g * per_group + i
            block = kv_buf[t].reshape(total_len, kvc)
            scores = (
                lax.dot_general(
                    q_buf[t], block, (((1,), (1,)), ((), ())), preferred_element_type=F32
                )
                * score_scale
            )
            live = lax.broadcasted_iota(jnp.int32, (heads, total_len), 1) < lengths[t]
            scores = jnp.where(live, scores, -1e30)
            peak = jnp.max(scores, -1, keepdims=True)
            prob = jnp.where(live, jnp.exp(scores - peak), 0.0)
            mass = jnp.sum(prob, -1, keepdims=True)
            acc[t] = jnp.dot(prob.astype(BF16), block[:, :lat], preferred_element_type=F32)
            peaks[t] = jnp.broadcast_to(peak, (heads, 128))
            masses[t] = jnp.broadcast_to(mass, (heads, 128))
            return carry

        lax.fori_loop(0, per_group, body, 0)

    local[2].wait()
    local[3].wait()
    gate = jnp.zeros((rows, wg.shape[1]), F32)
    upper = jnp.zeros((rows, wg.shape[1]), F32)
    square = jnp.zeros((rows, 1), F32)
    for turn in range(n_tp):
        b = tp_id(turn)
        for step in range(1, experts):
            peer = ex_id(step)
            arrival(arrived.at[peer, b], row_rsem.at[peer, b]).wait()
        wide = arrived[:, b].astype(F32).reshape(rows, d_loc)
        square = square + jnp.sum(wide * wide, -1, keepdims=True)
        block = (wide * gain_all[b]).astype(BF16)
        deep = pl.ds(pl.multiple_of(b * d_loc, d_loc & -d_loc), d_loc)
        gate = gate + jnp.dot(block, wg[deep], preferred_element_type=F32)
        upper = upper + jnp.dot(block, wu[deep], preferred_element_type=F32)
    scale = lax.rsqrt(square / d_all + epsilon)
    gate = gate * scale
    upper = upper * scale
    units = (gate / (1.0 + jnp.exp(-gate)) * upper).astype(BF16)
    local[4].wait()
    width = 512 if d_all % 512 == 0 else 128
    aligned = d_loc % 128 == 0
    if aligned:
        width = next(w for w in (896, 512, 384, 256, 128) if d_loc % w == 0)
        pieces = [
            (pl.multiple_of(tp_id(turn) * d_loc, 128), d_loc) for turn in (*range(1, n_tp), 0)
        ]
    else:
        middle = d_all // width // 2 * width
        pieces = [(0, middle), (middle, d_all - middle)]

    def columns(start, size):
        return pl.ds(pl.multiple_of(start, 128), size)

    for h, (first, size) in enumerate(pieces):
        for c in range(0, size, width):
            part = jnp.dot(units, wd[:, columns(first + c, width)], preferred_element_type=F32)
            ret_send[:, :, columns(first + c, width)] = part.reshape(
                experts, CAP, width
            ).astype(BF16)
        for step in range(1, experts):
            peer = ex_id(step)
            copy = pltpu.make_async_remote_copy(
                src_ref=ret_send.at[peer, :, columns(first, size)],
                dst_ref=ret.at[me, :, columns(first, size)],
                send_sem=ret_ssem.at[step, h],
                recv_sem=ret_rsem.at[me, h],
                device_id=ex_dev(peer),
                device_id_type=MESH,
            )
            copy.start()
            sends.append(copy)
    ret[me] = ret_send[me]

    def exchange(step):
        copy = tp_copy(
            rs_send.at[tp_id(step)], rs_recv.at[tp], rs_ssem.at[step], rs_rsem.at[tp], step
        )
        copy.start()
        sends.append(copy)

    for h, (first, size) in enumerate(pieces):
        for step in range(1, experts):
            peer = ex_id(step)
            arrival(ret.at[peer, :, columns(first, size)], ret_rsem.at[peer, h]).wait()
        for c in range(0, size, width):
            block = ret[:, :, columns(first + c, width)].astype(F32)
            block = block.reshape(rows, width).astype(BF16)
            part = jnp.dot(combine3, block, preferred_element_type=F32)
            part = part[:tokens] + (part[tokens : 2 * tokens] + part[2 * tokens : 3 * tokens])
            if aligned:
                rs_send[tp_id(h + 1), :, c : c + width] = part.astype(BF16)
            else:
                tsum[:, columns(first + c, width)] = part
        if aligned and h < n_tp - 1:
            exchange(h + 1)
        if h == 0:
            for g in range(GROUPS // 2):
                attend(g)
    if not aligned:
        for p in range(n_tp):
            rs_send[p] = tsum[:, p * d_loc : (p + 1) * d_loc].astype(BF16)
        for step in range(1, n_tp):
            exchange(step)
    rs_recv[tp] = rs_send[tp]
    local[5].wait()
    for step in range(1, n_tp):
        arrival(rs_recv.at[tp_id(step)], rs_rsem.at[tp_id(step)]).wait()
    moe = rs_recv[0].astype(F32)
    for p in range(1, n_tp):
        moe = moe + rs_recv[p].astype(F32)
    next_hidden = (hid_all[tp].astype(F32) + moe).astype(BF16)
    next_out[...] = next_hidden
    next_wide = next_hidden.astype(F32)
    square = jnp.sum(next_wide * next_wide, -1, keepdims=True)
    scaled = (next_wide * attn_gain[...].reshape(1, d_loc)).astype(BF16)
    kvp = up(kvc, 128)
    if kvp > kvc:
        key_send[:, kvp - 128 : kvp] = jnp.zeros((tokens, 128), F32)
    key_send[:, :kvc] = lax.dot_general(
        scaled, wk[...], (((1,), (1,)), ((), ())), preferred_element_type=F32
    )
    key_send[:, kvp : kvp + 128] = jnp.broadcast_to(square, (tokens, 128))
    for step in range(1, n_tp):
        copy = tp_copy(key_send, key_recv.at[tp], key_ssem.at[step], key_rsem.at[tp], step)
        copy.start()
        sends.append(copy)
    key_recv[tp] = key_send[...]
    for g in range(GROUPS // 2, GROUPS):
        attend(g)

    half = (kvc - lat) // 2
    lane = lax.broadcasted_iota(jnp.int32, (tokens, 2 * half), 1)
    pair = jnp.where(lane < half, lane, lane - half).astype(F32)
    freq = jnp.exp(pair * (-9.210340371976184 / half))
    row_id = lax.broadcasted_iota(jnp.int32, (tokens, 2 * half), 0)
    place = jnp.zeros((tokens, 2 * half), F32)
    for t in range(tokens):
        place = jnp.where(row_id == t, lengths[t].astype(F32), place)
    angle = place * freq
    cos_table = jnp.cos(angle)
    sin_table = jnp.where(lane < half, -1.0, 1.0) * jnp.sin(angle)

    for step in range(1, n_tp):
        arrival(key_recv.at[tp_id(step)], key_rsem.at[tp_id(step)]).wait()
    total = key_recv[0]
    for p in range(1, n_tp):
        total = total + key_recv[p]
    down = total * lax.rsqrt(total[:, kvp : kvp + 1] / d_all + epsilon)
    latent = down[:, :lat]
    latent = (
        latent
        * lax.rsqrt(jnp.mean(latent * latent, -1, keepdims=True) + epsilon)
        * kv_gain[...]
    )
    rope = down[:, lat:kvc]
    swapped = jnp.concatenate([rope[:, half:], rope[:, :half]], 1)
    rope = rope * cos_table + swapped * sin_table
    keys[:, :lat] = latent.astype(BF16).astype(F32)
    keys[:, lat:kvc] = rope.astype(BF16).astype(F32)

    def finish(t, carry):
        key = keys[pl.ds(t, 1), :]
        own = jnp.sum(q_buf[t].astype(F32) * key, -1, keepdims=True) * score_scale
        peak = peaks[t][:, :1]
        mass = masses[t][:, :1]
        top = jnp.maximum(peak, own)
        factor = jnp.exp(peak - top)
        own_prob = jnp.exp(own - top)
        inverse = 1.0 / (mass * factor + own_prob)
        own_b = own_prob.astype(BF16).astype(F32)
        latent_out[t] = (acc[t] * (factor * inverse) + (own_b * inverse) * key[:, :lat]).astype(
            BF16
        )
        return carry

    lax.fori_loop(0, tokens, finish, 0)
    for copy in sends:
        copy.wait_send()


def solution(mesh):
    n_tp, n_ep, n_mb = mesh.shape["tp"], mesh.shape["ep"], mesh.shape["mb"]
    experts = n_ep * n_mb

    def local(
        hidden,
        moe_gain,
        expert_ids,
        slots,
        affinity,
        w_gate,
        w_up,
        w_down,
        attn_gain,
        w_dkv,
        kv_gain,
        queries,
        cache,
        lengths,
    ):
        tokens, d_loc = hidden.shape
        d_all = d_loc * n_tp
        heads, kvc = queries.shape[1:]
        span = cache.shape[1]
        lat = kv_gain.shape[0]
        hid_dim = w_gate.shape[2]
        wide = up(kvc, 128) + 128
        any_space = pl.BlockSpec(memory_space=pl.ANY)
        vmem = pl.BlockSpec(memory_space=pltpu.VMEM)
        smem = pl.BlockSpec(memory_space=pltpu.SMEM)
        dma = pltpu.SemaphoreType.DMA
        return pl.pallas_call(
            functools.partial(kernel, n_tp, n_ep, n_mb),
            out_shape=(
                jax.ShapeDtypeStruct((tokens, d_loc), BF16),
                jax.ShapeDtypeStruct((tokens, heads, lat), BF16),
            ),
            in_specs=[
                any_space,
                vmem,
                vmem,
                vmem,
                vmem,
                any_space,
                any_space,
                any_space,
                vmem,
                any_space,
                vmem,
                any_space,
                any_space,
                smem,
            ],
            out_specs=(vmem, vmem),
            scratch_shapes=[
                pltpu.VMEM((n_tp, tokens, d_loc), BF16),
                pltpu.VMEM((n_tp, 1, d_loc), F32),
                pltpu.VMEM((experts, n_tp, CAP, d_loc), BF16),
                pltpu.VMEM((experts, n_tp, CAP, d_loc), BF16),
                pltpu.VMEM((d_all, hid_dim), BF16),
                pltpu.VMEM((d_all, hid_dim), BF16),
                pltpu.VMEM((hid_dim, d_all), BF16),
                pltpu.VMEM((kvc, d_loc), BF16),
                pltpu.VMEM((experts, CAP, d_all), BF16),
                pltpu.VMEM((experts, CAP, d_all), BF16),
                pltpu.VMEM((tokens, d_all), F32),
                pltpu.VMEM((n_tp, tokens, d_loc), BF16),
                pltpu.VMEM((n_tp, tokens, d_loc), BF16),
                pltpu.VMEM((tokens, wide), F32),
                pltpu.VMEM((n_tp, tokens, wide), F32),
                pltpu.VMEM((tokens, heads, kvc), BF16),
                pltpu.VMEM((tokens, n_tp, span, kvc), BF16),
                pltpu.VMEM((tokens, heads, lat), F32),
                pltpu.VMEM((tokens, heads, 128), F32),
                pltpu.VMEM((tokens, heads, 128), F32),
                pltpu.VMEM((tokens, kvc), F32),
                dma((6,)),
                dma,
                dma((n_tp,)),
                dma((n_tp,)),
                dma((n_tp,)),
                dma((n_tp,)),
                dma((n_tp, GROUPS)),
                dma((n_tp, GROUPS)),
                dma((experts, n_tp)),
                dma((experts, n_tp)),
                dma((experts, max(2, n_tp))),
                dma((experts, max(2, n_tp))),
                dma((n_tp,)),
                dma((n_tp,)),
                dma((n_tp,)),
                dma((n_tp,)),
            ],
            compiler_params=pltpu.CompilerParams(
                collective_id=0, has_side_effects=True, vmem_limit_bytes=60 * 1024 * 1024
            ),
        )(
            hidden,
            moe_gain,
            expert_ids.T,
            slots.T,
            affinity.T,
            w_gate,
            w_up,
            w_down,
            attn_gain,
            w_dkv.T,
            kv_gain[None],
            queries,
            cache,
            lengths,
        )

    return jax.shard_map(
        local,
        mesh=mesh,
        in_specs=(
            P(("grp", "ep", "mb"), "tp"),
            P("tp"),
            P(("grp", "ep", "mb"), None),
            P(("grp", "ep", "mb"), None),
            P(("grp", "ep", "mb"), None),
            P(("ep", "mb"), None, "tp"),
            P(("ep", "mb"), None, "tp"),
            P(("ep", "mb"), "tp", None),
            P("tp"),
            P("tp", None),
            P(),
            P(("grp", "ep", "mb"), "tp", None),
            P(("grp", "ep", "mb"), "tp", None),
            P(("grp", "ep", "mb")),
        ),
        out_specs=(P(("grp", "ep", "mb"), "tp"), P(("grp", "ep", "mb"), "tp", None)),
        check_vma=False,
    )
```

profile of v0, /device:TPU:0, one launch (start us, length us, event | category | flops | bytes accessed | tf_op | source)
XLA Modules:
  0.0 52.6 jit_solution(12637204748209121876)
XLA Ops:
  0.6 48.6 %shard_map.149 = (bf16[16,1792]{1,0:T(8,128)(2,1)}, bf16[16,32,512]{2,1,0:T(8,128)(2,1)}) custom-call(bf16[16,1792]{1,0:T(8,128)(2,1)} %hidden.1, f32[1792]{0:T(1024)} %moe_gain.1, s32[8,16]{1,0:T(8,128)} %bitcast.6, s32[8,16]{1,0:T(8,128)} %bitcast.7, f32[8,16]{1,0:T(8,128)} %bitcast.8, bf16[1,3584,512]{2,1,0:T(8,128)(2,1)} %w_gate.1, ...), custom_call_target="tpu_custom_call" | custom-call | tf_op jit(solution)/shard_map/pallas_call | solution.py:429
  49.3 1.4 %copy.18 = bf16[16,1792]{1,0:T(8,128)(2,1)} copy(bf16[16,1792]{1,0:T(8,128)(2,1)} %get-tuple-element.4) | data formatting | bytes 114688
  50.7 1.9 %copy.19 = bf16[16,32,512]{2,1,0:T(8,128)(2,1)} copy(bf16[16,32,512]{2,1,0:T(8,128)(2,1)} %get-tuple-element.5) | data formatting | bytes 1048576
where the time goes:
time: 52.9 us; the launch traced here: 52.6 us
  Pallas kernels  48.6 us (92%)
  local copies, waits for them, and re-layouts  3.33 us (6%)
  between operations  0.64 us (1%)
    pallas_call x1, Pallas kernels, local(): pl.pallas_call(functools.partial(kernel, n_tp, n_ep, n_mb), out_shape=(ja...  48.6 us
    unnamed x2, local copies, waits for them, and re-layouts  3.33 us

commit v1 on v0

--- a/solution.py
+++ b/solution.py
@@ -429,8 +429,8 @@
         return pl.pallas_call(
             functools.partial(kernel, n_tp, n_ep, n_mb),
             out_shape=(
-                jax.ShapeDtypeStruct((tokens, d_loc), BF16),
-                jax.ShapeDtypeStruct((tokens, heads, lat), BF16),
+                pltpu.VMEM((tokens, d_loc), BF16),
+                pltpu.VMEM((tokens, heads, lat), BF16),
             ),
             in_specs=[
                 any_space,

time: 52.9 us -> 50.1 us (0.947)
  local copies, waits for them, and re-layouts: 3.33 us -> 1.42 us
  Pallas kernels: 48.6 us -> 47.8 us
    unnamed x2, local copies, waits for them, and re-layouts: 3.33 us -> 1.42 us
    pallas_call x1, Pallas kernels: 48.6 us -> 47.8 us  [local(): pl.pallas_call(functools.partial(kernel, n_tp, n_ep, n_mb), out_shape=(pl...]
where the time goes in v1:
time: 50.1 us; the launch traced here: 49.9 us
  Pallas kernels  47.8 us (95%)
  local copies, waits for them, and re-layouts  1.42 us (3%)
  between operations  0.64 us (1%)
    pallas_call x1, Pallas kernels, local(): pl.pallas_call(functools.partial(kernel, n_tp, n_ep, n_mb), out_shape=(pl...  47.8 us
    unnamed x2, local copies, waits for them, and re-layouts  1.42 us

profile of v1, /device:TPU:0, one launch (start us, length us, event | category | flops | bytes accessed | tf_op | source)
XLA Modules:
  0.0 49.9 jit_solution(17097633176764562729)
XLA Ops:
  0.6 47.8 %shard_map.149 = (bf16[16,1792]{1,0:T(8,128)(2,1)S(1)}, bf16[16,32,512]{2,1,0:T(8,128)(2,1)S(1)}) custom-call(bf16[16,1792]{1,0:T(8,128)(2,1)} %hidden.1, f32[1792]{0:T(1024)} %moe_gain.1, s32[8,16]{1,0:T(8,128)} %bitcast.6, s32[8,16]{1,0:T(8,128)} %bitcast.7, f32[8,16]{1,0:T(8,128)} %bitcast.8, bf16[1,3584,512]{2,1,0:T(8,128)(2,1)} %w_gate.1, ...), custom_call_target="tpu_custom_call" | custom-call | tf_op jit(solution)/shard_map/pallas_call | solution.py:429
  48.5 0.6 %copy.18 = bf16[16,1792]{1,0:T(8,128)(2,1)} copy(bf16[16,1792]{1,0:T(8,128)(2,1)S(1)} %get-tuple-element.2) | data formatting | bytes 114688
  49.1 0.8 %copy.19 = bf16[16,32,512]{2,1,0:T(8,128)(2,1)} copy(bf16[16,32,512]{2,1,0:T(8,128)(2,1)S(1)} %get-tuple-element.3) | data formatting | bytes 1048576

commit v2 on v1

--- a/solution.py
+++ b/solution.py
@@ -8,10 +8,11 @@
 from jax.sharding import PartitionSpec as P
 
 CAP = 8
-GROUPS = 4
+AHEAD = 3
 epsilon = 1e-06
 route_scale = 2.5
 score_scale = 192.0 ** (-0.5)
+STOPS = (2, 5, 10, 13)
 MESH = pl.DeviceIdType.MESH
 F32 = jnp.float32
 BF16 = jnp.bfloat16
@@ -19,6 +20,16 @@
 
 def up(value, step):
     return -(-value // step) * step
+
+
+def split3(value, width):
+    high = value.astype(BF16)
+    rest = value - high.astype(F32)
+    mid = rest.astype(BF16)
+    low = (rest - mid.astype(F32)).astype(BF16)
+    lane = lax.broadcasted_iota(jnp.int32, (value.shape[0], width), 1)
+    parts = jnp.where(lane == 1, mid.astype(F32), jnp.where(lane == 2, low.astype(F32), 0.0))
+    return jnp.where(lane == 0, high.astype(F32), parts).astype(BF16)
 
 
 def kernel(
@@ -62,6 +73,8 @@
     peaks,
     masses,
     keys,
+    old_part,
+    own_part,
     load_sem,
     kv_load_sem,
     hid_ssem,
@@ -84,7 +97,6 @@
     d_all = d_loc * n_tp
     lat = kv_gain.shape[1]
     kvc = cache.shape[2]
-    per_group = tokens // GROUPS
     tp = lax.axis_index("tp")
     me = lax.axis_index("ep") * n_mb + lax.axis_index("mb")
 
@@ -96,7 +108,6 @@
 
     def ex_dev(index):
         return {"ep": index // n_mb, "mb": lax.rem(index, n_mb)}
-
     local = [
         pltpu.make_async_copy(hidden, hid_all.at[tp], load_sem.at[0]),
         pltpu.make_async_copy(queries, q_buf, load_sem.at[1]),
@@ -107,6 +118,7 @@
     ]
     kv_load = pltpu.make_async_copy(cache, kv_buf.at[:, tp], kv_load_sem)
     local[0].start()
+    kv_load.start()
     gain_all[tp] = moe_gain[...].reshape(1, d_loc)
 
     barrier = pltpu.get_barrier_semaphore()
@@ -152,9 +164,11 @@
             copy.start()
             sends.append(copy)
         arrived[me, block] = send[me, block]
-
     local[0].wait()
     pick(tp)
+    kv_load.wait()
+    for copy in local[1:]:
+        copy.start()
     pl.semaphore_wait(barrier, n_tp - 1 + experts - 1)
 
     def tp_copy(src, dst, ssem, rsem, step):
@@ -169,31 +183,28 @@
 
     def arrival(dst, rsem):
         return pltpu.make_async_copy(dst, dst, rsem)
-
     sends = []
     for step in range(1, n_tp):
         for src, dst, ssem, rsem in (
-            (hidden, hid_all, hid_ssem, hid_rsem),
+            (hid_all.at[tp], hid_all, hid_ssem, hid_rsem),
             (gain_all.at[tp], gain_all, gain_ssem, gain_rsem),
         ):
             copy = tp_copy(src, dst.at[tp], ssem.at[step], rsem.at[tp], step)
             copy.start()
             sends.append(copy)
     ship(tp, 0)
-    for g in range(GROUPS):
-        span = pl.ds(g * per_group, per_group)
+
+    def cache_copy(t, step):
+        return tp_copy(
+            kv_buf.at[t, tp], kv_buf.at[t, tp], kv_ssem.at[step, t], kv_rsem.at[tp, t], step
+        )
+
+    def feed(t):
         for step in range(1, n_tp):
-            copy = tp_copy(
-                cache.at[span], kv_buf.at[span, tp], kv_ssem.at[step, g], kv_rsem.at[tp, g], step
-            )
-            copy.start()
-            sends.append(copy)
-    for copy in local[1:4]:
-        copy.start()
-    kv_load.start()
-    for copy in local[4:]:
-        copy.start()
-
+            cache_copy(t, step).start()
+
+    for t in range(AHEAD):
+        feed(t)
     for step in range(1, n_tp):
         arrival(hid_all.at[tp_id(step)], hid_rsem.at[tp_id(step)]).wait()
         arrival(gain_all.at[tp_id(step)], gain_rsem.at[tp_id(step)]).wait()
@@ -202,18 +213,19 @@
         ship(tp_id(turn), turn)
 
     local[1].wait()
-    kv_load.wait()
     heads = queries.shape[1]
     span_len = cache.shape[1]
     total_len = n_tp * span_len
 
-    def attend(g):
-        span = pl.ds(g * per_group, per_group)
-        for step in range(1, n_tp):
-            arrival(kv_buf.at[span, tp_id(step)], kv_rsem.at[tp_id(step), g]).wait()
-
-        def body(i, carry):
-            t = g * per_group + i
+    def attend(first, last):
+        def body(t, carry):
+            for step in range(1, n_tp):
+                arrival(kv_buf.at[t, tp_id(step)], kv_rsem.at[tp_id(step), t]).wait()
+
+            @pl.when(t + AHEAD < tokens)
+            def _():
+                feed(t + AHEAD)
+
             block = kv_buf[t].reshape(total_len, kvc)
             scores = (
                 lax.dot_general(
@@ -231,8 +243,10 @@
             masses[t] = jnp.broadcast_to(mass, (heads, 128))
             return carry
 
-        lax.fori_loop(0, per_group, body, 0)
-
+        lax.fori_loop(first, last, body, 0)
+
+    stops = [tokens * n // 16 for n in STOPS]
+    attend(0, stops[0])
     local[2].wait()
     local[3].wait()
     gate = jnp.zeros((rows, wg.shape[1]), F32)
@@ -240,6 +254,8 @@
     square = jnp.zeros((rows, 1), F32)
     for turn in range(n_tp):
         b = tp_id(turn)
+        if turn == n_tp - 1:
+            attend(stops[0], stops[1])
         for step in range(1, experts):
             peer = ex_id(step)
             arrival(arrived.at[peer, b], row_rsem.at[peer, b]).wait()
@@ -296,6 +312,8 @@
         sends.append(copy)
 
     for h, (first, size) in enumerate(pieces):
+        if h < 2:
+            attend(stops[h + 1], stops[h + 2])
         for step in range(1, experts):
             peer = ex_id(step)
             arrival(ret.at[peer, :, columns(first, size)], ret_rsem.at[peer, h]).wait()
@@ -310,9 +328,6 @@
                 tsum[:, columns(first + c, width)] = part
         if aligned and h < n_tp - 1:
             exchange(h + 1)
-        if h == 0:
-            for g in range(GROUPS // 2):
-                attend(g)
     if not aligned:
         for p in range(n_tp):
             rs_send[p] = tsum[:, p * d_loc : (p + 1) * d_loc].astype(BF16)
@@ -330,21 +345,19 @@
     next_wide = next_hidden.astype(F32)
     square = jnp.sum(next_wide * next_wide, -1, keepdims=True)
     scaled = (next_wide * attn_gain[...].reshape(1, d_loc)).astype(BF16)
-    kvp = up(kvc, 128)
-    if kvp > kvc:
-        key_send[:, kvp - 128 : kvp] = jnp.zeros((tokens, 128), F32)
-    key_send[:, :kvc] = lax.dot_general(
+    kvp = up(kvc + 3, 128)
+    tail = kvp - kvc
+    part = lax.dot_general(
         scaled, wk[...], (((1,), (1,)), ((), ())), preferred_element_type=F32
     )
-    key_send[:, kvp : kvp + 128] = jnp.broadcast_to(square, (tokens, 128))
+    key_send[:, :kvc] = part.astype(BF16)
+    key_send[:, kvc:kvp] = split3(square, tail)
     for step in range(1, n_tp):
         copy = tp_copy(key_send, key_recv.at[tp], key_ssem.at[step], key_rsem.at[tp], step)
         copy.start()
         sends.append(copy)
     key_recv[tp] = key_send[...]
-    for g in range(GROUPS // 2, GROUPS):
-        attend(g)
-
+    attend(stops[3], tokens)
     half = (kvc - lat) // 2
     lane = lax.broadcasted_iota(jnp.int32, (tokens, 2 * half), 1)
     pair = jnp.where(lane < half, lane, lane - half).astype(F32)
@@ -356,13 +369,13 @@
     angle = place * freq
     cos_table = jnp.cos(angle)
     sin_table = jnp.where(lane < half, -1.0, 1.0) * jnp.sin(angle)
-
     for step in range(1, n_tp):
         arrival(key_recv.at[tp_id(step)], key_rsem.at[tp_id(step)]).wait()
-    total = key_recv[0]
+    total = key_recv[0].astype(F32)
     for p in range(1, n_tp):
-        total = total + key_recv[p]
-    down = total * lax.rsqrt(total[:, kvp : kvp + 1] / d_all + epsilon)
+        total = total + key_recv[p].astype(F32)
+    square = jnp.sum(total[:, kvc:], -1, keepdims=True)
+    down = total * lax.rsqrt(square / d_all + epsilon)
     latent = down[:, :lat]
     latent = (
         latent
@@ -372,27 +385,40 @@
     rope = down[:, lat:kvc]
     swapped = jnp.concatenate([rope[:, half:], rope[:, :half]], 1)
     rope = rope * cos_table + swapped * sin_table
-    keys[:, :lat] = latent.astype(BF16).astype(F32)
-    keys[:, lat:kvc] = rope.astype(BF16).astype(F32)
-
-    def finish(t, carry):
-        key = keys[pl.ds(t, 1), :]
-        own = jnp.sum(q_buf[t].astype(F32) * key, -1, keepdims=True) * score_scale
-        peak = peaks[t][:, :1]
-        mass = masses[t][:, :1]
-        top = jnp.maximum(peak, own)
-        factor = jnp.exp(peak - top)
-        own_prob = jnp.exp(own - top)
-        inverse = 1.0 / (mass * factor + own_prob)
-        own_b = own_prob.astype(BF16).astype(F32)
-        latent_out[t] = (acc[t] * (factor * inverse) + (own_b * inverse) * key[:, :lat]).astype(
-            BF16
-        )
-        return carry
-
-    lax.fori_loop(0, tokens, finish, 0)
+    keys[:, :lat] = latent.astype(BF16)
+    keys[:, lat:kvc] = rope.astype(BF16)
+    pairs = tokens * heads
+    own = lax.dot_general(
+        q_buf[...].reshape(pairs, kvc),
+        keys[...],
+        (((1,), (1,)), ((), ())),
+        preferred_element_type=F32,
+    )
+    owner = lax.broadcasted_iota(jnp.int32, (pairs, tokens), 0) // heads
+    mine = owner == lax.broadcasted_iota(jnp.int32, (pairs, tokens), 1)
+    own = jnp.sum(jnp.where(mine, own, 0.0), -1, keepdims=True) * score_scale
+    own = jnp.broadcast_to(own, (pairs, 128))
+    peak = peaks[...].reshape(pairs, 128)
+    top = jnp.maximum(peak, own)
+    factor = jnp.exp(peak - top)
+    own_prob = jnp.exp(own - top)
+    inverse = 1.0 / (masses[...].reshape(pairs, 128) * factor + own_prob)
+    old_part[...] = (factor * inverse).reshape(tokens, heads, 128)
+    own_part[...] = (own_prob.astype(BF16).astype(F32) * inverse).reshape(tokens, heads, 128)
+    for t in range(tokens):
+        for c in range(0, lat, 128):
+            value = acc[t, :, c : c + 128] * old_part[t]
+            key = keys[t : t + 1, c : c + 128].astype(F32)
+            latent_out[t, :, c : c + 128] = (value + own_part[t] * key).astype(BF16)
     for copy in sends:
         copy.wait_send()
+
+    def drain(t, carry):
+        for step in range(1, n_tp):
+            cache_copy(t, step).wait_send()
+        return carry
+
+    lax.fori_loop(0, tokens, drain, 0)
 
 
 def solution(mesh):
@@ -421,7 +447,7 @@
         span = cache.shape[1]
         lat = kv_gain.shape[0]
         hid_dim = w_gate.shape[2]
-        wide = up(kvc, 128) + 128
+        wide = up(kvc + 3, 128)
         any_space = pl.BlockSpec(memory_space=pl.ANY)
         vmem = pl.BlockSpec(memory_space=pltpu.VMEM)
         smem = pl.BlockSpec(memory_space=pltpu.SMEM)
@@ -463,22 +489,24 @@
                 pltpu.VMEM((tokens, d_all), F32),
                 pltpu.VMEM((n_tp, tokens, d_loc), BF16),
                 pltpu.VMEM((n_tp, tokens, d_loc), BF16),
-                pltpu.VMEM((tokens, wide), F32),
-                pltpu.VMEM((n_tp, tokens, wide), F32),
+                pltpu.VMEM((tokens, wide), BF16),
+                pltpu.VMEM((n_tp, tokens, wide), BF16),
                 pltpu.VMEM((tokens, heads, kvc), BF16),
                 pltpu.VMEM((tokens, n_tp, span, kvc), BF16),
                 pltpu.VMEM((tokens, heads, lat), F32),
                 pltpu.VMEM((tokens, heads, 128), F32),
                 pltpu.VMEM((tokens, heads, 128), F32),
-                pltpu.VMEM((tokens, kvc), F32),
+                pltpu.VMEM((tokens, kvc), BF16),
+                pltpu.VMEM((tokens, heads, 128), F32),
+                pltpu.VMEM((tokens, heads, 128), F32),
                 dma((6,)),
                 dma,
                 dma((n_tp,)),
                 dma((n_tp,)),
                 dma((n_tp,)),
                 dma((n_tp,)),
-                dma((n_tp, GROUPS)),
-                dma((n_tp, GROUPS)),
+                dma((n_tp, tokens)),
+                dma((n_tp, tokens)),
                 dma((experts, n_tp)),
                 dma((experts, n_tp)),
                 dma((experts, max(2, n_tp))),

time: 50.1 us -> 44.4 us (0.89)
  Pallas kernels: 47.8 us -> 42.1 us
    pallas_call x1, Pallas kernels: 47.8 us -> 42.1 us  [local(): pl.pallas_call(functools.partial(kernel, n_tp, n_ep, n_mb), out_shape=(pl...]
where the time goes in v2:
time: 44.4 us; the launch traced here: 44.2 us
  Pallas kernels  42.1 us (95%)
  local copies, waits for them, and re-layouts  1.42 us (3%)
  between operations  0.64 us (1%)
    pallas_call x1, Pallas kernels, local(): pl.pallas_call(functools.partial(kernel, n_tp, n_ep, n_mb), out_shape=(pl...  42.1 us
    unnamed x2, local copies, waits for them, and re-layouts  1.42 us

profile of v2, /device:TPU:0, one launch (start us, length us, event | category | flops | bytes accessed | tf_op | source)
XLA Modules:
  0.0 44.2 jit_solution(4653922464643884413)
XLA Ops:
  0.6 42.1 %shard_map.149 = (bf16[16,1792]{1,0:T(8,128)(2,1)S(1)}, bf16[16,32,512]{2,1,0:T(8,128)(2,1)S(1)}) custom-call(bf16[16,1792]{1,0:T(8,128)(2,1)} %hidden.1, f32[1792]{0:T(1024)} %moe_gain.1, s32[8,16]{1,0:T(8,128)} %bitcast.6, s32[8,16]{1,0:T(8,128)} %bitcast.7, f32[8,16]{1,0:T(8,128)} %bitcast.8, bf16[1,3584,512]{2,1,0:T(8,128)(2,1)} %w_gate.1, ...), custom_call_target="tpu_custom_call" | custom-call | tf_op jit(solution)/shard_map/pallas_call | solution.py:455
  42.8 0.6 %copy.18 = bf16[16,1792]{1,0:T(8,128)(2,1)} copy(bf16[16,1792]{1,0:T(8,128)(2,1)S(1)} %get-tuple-element.2) | data formatting | bytes 114688
  43.4 0.8 %copy.19 = bf16[16,32,512]{2,1,0:T(8,128)(2,1)} copy(bf16[16,32,512]{2,1,0:T(8,128)(2,1)S(1)} %get-tuple-element.3) | data formatting | bytes 1048576

commit v3 on v2

--- a/solution.py
+++ b/solution.py
@@ -37,19 +37,19 @@
     n_ep,
     n_mb,
     hidden,
-    moe_gain,
-    ids,
-    slots,
-    affinity,
+    moe_gain_in,
+    ids_in,
+    slots_in,
+    affinity_in,
     w_gate,
     w_up,
     w_down,
-    attn_gain,
+    attn_gain_in,
     w_dkv,
-    kv_gain,
+    kv_gain_in,
     queries,
     cache,
-    lengths,
+    lengths_in,
     next_out,
     latent_out,
     hid_all,
@@ -75,6 +75,15 @@
     keys,
     old_part,
     own_part,
+    moe_gain,
+    ids,
+    slots,
+    affinity,
+    attn_gain,
+    kv_gain,
+    lengths,
+    small_sem,
+    near_sem,
     load_sem,
     kv_load_sem,
     hid_ssem,
@@ -98,6 +107,7 @@
     lat = kv_gain.shape[1]
     kvc = cache.shape[2]
     tp = lax.axis_index("tp")
+    chained = 1 < n_ep <= 4
     me = lax.axis_index("ep") * n_mb + lax.axis_index("mb")
 
     def tp_id(step):
@@ -117,15 +127,46 @@
         pltpu.make_async_copy(w_dkv, wk, load_sem.at[5]),
     ]
     kv_load = pltpu.make_async_copy(cache, kv_buf.at[:, tp], kv_load_sem)
+    small = [
+        pltpu.make_async_copy(src, dst, small_sem.at[i])
+        for i, (src, dst) in enumerate(
+            (
+                (slots_in, slots),
+                (ids_in, ids),
+                (affinity_in, affinity),
+                (moe_gain_in, moe_gain),
+                (attn_gain_in, attn_gain),
+                (kv_gain_in, kv_gain),
+                (lengths_in, lengths),
+            )
+        )
+    ]
+    for copy in small[:4]:
+        copy.start()
     local[0].start()
     kv_load.start()
+    for copy in small[4:]:
+        copy.start()
+
+    ep, mb = lax.axis_index("ep"), lax.axis_index("mb")
+    barrier = pltpu.get_barrier_semaphore()
+
+    def hello(sem, ids):
+        pl.semaphore_signal(sem, inc=1, device_id=ids, device_id_type=MESH)
+
+    for step in range(1, n_tp):
+        hello(barrier, {"tp": tp_id(step)})
+    if chained:
+        for step in range(1, n_mb):
+            hello(barrier, {"mb": lax.rem(mb + step, n_mb)})
+        greeted = n_tp - 1 + n_mb - 1 + n_mb * jnp.minimum(ep, 1)
+    else:
+        for step in range(1, experts):
+            hello(barrier, ex_dev(ex_id(step)))
+        greeted = n_tp - 1 + experts - 1
+    for copy in small[:4]:
+        copy.wait()
     gain_all[tp] = moe_gain[...].reshape(1, d_loc)
-
-    barrier = pltpu.get_barrier_semaphore()
-    for step in range(1, n_tp):
-        pl.semaphore_signal(barrier, inc=1, device_id={"tp": tp_id(step)}, device_id_type=MESH)
-    for step in range(1, experts):
-        pl.semaphore_signal(barrier, inc=1, device_id=ex_dev(ex_id(step)), device_id_type=MESH)
     kept = slots[...] < CAP
     aff = affinity[...]
     weight = route_scale * aff / jnp.sum(aff, 0, keepdims=True) * kept.astype(F32)
@@ -150,26 +191,50 @@
         picked = jnp.dot(dispatch, hid_all[block], preferred_element_type=F32)
         send[:, block] = picked.reshape(experts, CAP, d_loc).astype(BF16)
 
-    def ship(block, turn):
-        for step in range(1, experts):
-            peer = ex_id(step)
-            copy = pltpu.make_async_remote_copy(
-                src_ref=send.at[peer, block],
-                dst_ref=arrived.at[me, block],
-                send_sem=row_ssem.at[step, turn],
-                recv_sem=row_rsem.at[me, block],
-                device_id=ex_dev(peer),
-                device_id_type=MESH,
-            )
-            copy.start()
-            sends.append(copy)
+    def row_copy(peer, block):
+        return pltpu.make_async_remote_copy(
+            src_ref=send.at[peer, block],
+            dst_ref=arrived.at[me, block],
+            send_sem=row_ssem.at[peer, block],
+            recv_sem=row_rsem.at[me, block],
+            device_id=ex_dev(peer),
+            device_id_type=MESH,
+        )
+
+    def ship_to(ep_index, block):
+        for m in range(n_mb):
+            row_copy(ep_index * n_mb + m, block).start()
+
+    def ship_near(block):
         arrived[me, block] = send[me, block]
+        for step in range(1, n_mb):
+            row_copy(ep * n_mb + lax.rem(mb + step, n_mb), block).start()
+
+    def ship(block):
+        ship_near(block)
+        for far in range(1, n_ep):
+            pl.when(ep >= far)(functools.partial(ship_to, ep - far, block))
+            pl.when(ep + far < n_ep)(functools.partial(ship_to, ep + far, block))
     local[0].wait()
     pick(tp)
     kv_load.wait()
     for copy in local[1:]:
         copy.start()
-    pl.semaphore_wait(barrier, n_tp - 1 + experts - 1)
+    pl.semaphore_wait(barrier, greeted)
+    if chained:
+
+        @pl.when(ep + 1 < n_ep)
+        def _():
+            for m in range(n_mb):
+                hello(barrier, {"ep": ep + 1, "mb": m})
+
+        for far in range(1, n_ep):
+
+            @pl.when(ep >= far)
+            def _():
+                for m in range(n_mb):
+                    hello(near_sem.at[far], {"ep": ep - far, "mb": m})
+
 
     def tp_copy(src, dst, ssem, rsem, step):
         return pltpu.make_async_remote_copy(
@@ -192,7 +257,6 @@
             copy = tp_copy(src, dst.at[tp], ssem.at[step], rsem.at[tp], step)
             copy.start()
             sends.append(copy)
-    ship(tp, 0)
 
     def cache_copy(t, step):
         return tp_copy(
@@ -205,12 +269,24 @@
 
     for t in range(AHEAD):
         feed(t)
+    if chained:
+        ship_near(tp)
+        for far in range(1, n_ep):
+            pl.when(ep >= far)(functools.partial(ship_to, ep - far, tp))
+        for far in range(1, n_ep):
+
+            @pl.when(ep + far < n_ep)
+            def _():
+                pl.semaphore_wait(near_sem.at[far], n_mb)
+                ship_to(ep + far, tp)
+    else:
+        ship(tp)
     for step in range(1, n_tp):
         arrival(hid_all.at[tp_id(step)], hid_rsem.at[tp_id(step)]).wait()
         arrival(gain_all.at[tp_id(step)], gain_rsem.at[tp_id(step)]).wait()
     for turn in range(1, n_tp):
         pick(tp_id(turn))
-        ship(tp_id(turn), turn)
+        ship(tp_id(turn))
 
     local[1].wait()
     heads = queries.shape[1]
@@ -245,6 +321,8 @@
 
         lax.fori_loop(first, last, body, 0)
 
+    for copy in small[4:]:
+        copy.wait()
     stops = [tokens * n // 16 for n in STOPS]
     attend(0, stops[0])
     local[2].wait()
@@ -413,6 +491,10 @@
     for copy in sends:
         copy.wait_send()
 
+    for step in range(1, experts):
+        for block in range(n_tp):
+            row_copy(ex_id(step), block).wait_send()
+
     def drain(t, carry):
         for step in range(1, n_tp):
             cache_copy(t, step).wait_send()
@@ -447,10 +529,10 @@
         span = cache.shape[1]
         lat = kv_gain.shape[0]
         hid_dim = w_gate.shape[2]
+        top = expert_ids.shape[1]
         wide = up(kvc + 3, 128)
         any_space = pl.BlockSpec(memory_space=pl.ANY)
         vmem = pl.BlockSpec(memory_space=pltpu.VMEM)
-        smem = pl.BlockSpec(memory_space=pltpu.SMEM)
         dma = pltpu.SemaphoreType.DMA
         return pl.pallas_call(
             functools.partial(kernel, n_tp, n_ep, n_mb),
@@ -458,22 +540,7 @@
                 pltpu.VMEM((tokens, d_loc), BF16),
                 pltpu.VMEM((tokens, heads, lat), BF16),
             ),
-            in_specs=[
-                any_space,
-                vmem,
-                vmem,
-                vmem,
-                vmem,
-                any_space,
-                any_space,
-                any_space,
-                vmem,
-                any_space,
-                vmem,
-                any_space,
-                any_space,
-                smem,
-            ],
+            in_specs=[any_space] * 14,
             out_specs=(vmem, vmem),
             scratch_shapes=[
                 pltpu.VMEM((n_tp, tokens, d_loc), BF16),
@@ -499,6 +566,15 @@
                 pltpu.VMEM((tokens, kvc), BF16),
                 pltpu.VMEM((tokens, heads, 128), F32),
                 pltpu.VMEM((tokens, heads, 128), F32),
+                pltpu.VMEM((d_loc,), F32),
+                pltpu.VMEM((top, tokens), jnp.int32),
+                pltpu.VMEM((top, tokens), jnp.int32),
+                pltpu.VMEM((top, tokens), F32),
+                pltpu.VMEM((d_loc,), F32),
+                pltpu.VMEM((1, lat), F32),
+                pltpu.SMEM((tokens,), jnp.int32),
+                dma((7,)),
+                pltpu.SemaphoreType.REGULAR((n_ep,)),
                 dma((6,)),
                 dma,
                 dma((n_tp,)),

time: 44.4 us -> 42.3 us (0.953)
  Pallas kernels: 42.1 us -> 40.1 us
    pallas_call x1, Pallas kernels: 42.1 us -> 40.1 us  [local(): pl.pallas_call(functools.partial(kernel, n_tp, n_ep, n_mb), out_shape=(pl...]
where the time goes in v3:
time: 42.3 us; the launch traced here: 42.2 us
  Pallas kernels  40.1 us (95%)
  local copies, waits for them, and re-layouts  1.42 us (3%)
  between operations  0.64 us (2%)
    pallas_call x1, Pallas kernels, local(): pl.pallas_call(functools.partial(kernel, n_tp, n_ep, n_mb), out_shape=(pl...  40.1 us
    unnamed x2, local copies, waits for them, and re-layouts  1.42 us

profile of v3, /device:TPU:0, one launch (start us, length us, event | category | flops | bytes accessed | tf_op | source)
XLA Modules:
  0.0 42.2 jit_solution(16785587197415516053)
XLA Ops:
  0.6 40.1 %shard_map.149 = (bf16[16,1792]{1,0:T(8,128)(2,1)S(1)}, bf16[16,32,512]{2,1,0:T(8,128)(2,1)S(1)}) custom-call(bf16[16,1792]{1,0:T(8,128)(2,1)} %hidden.1, f32[1792]{0:T(1024)} %moe_gain_in.1, s32[8,16]{1,0:T(8,128)} %bitcast.6, s32[8,16]{1,0:T(8,128)} %bitcast.7, f32[8,16]{1,0:T(8,128)} %bitcast.8, bf16[1,3584,512]{2,1,0:T(8,128)(2,1)} %w_gate.1, ...), custom_call_target="tpu_custom_call" | custom-call | tf_op jit(solution)/shard_map/pallas_call | solution.py:537
  40.7 0.6 %copy.18 = bf16[16,1792]{1,0:T(8,128)(2,1)} copy(bf16[16,1792]{1,0:T(8,128)(2,1)S(1)} %get-tuple-element.2) | data formatting | bytes 114688
  41.4 0.8 %copy.19 = bf16[16,32,512]{2,1,0:T(8,128)(2,1)} copy(bf16[16,32,512]{2,1,0:T(8,128)(2,1)S(1)} %get-tuple-element.3) | data formatting | bytes 1048576

commit v4 on v3

--- a/solution.py
+++ b/solution.py
@@ -12,7 +12,7 @@
 epsilon = 1e-06
 route_scale = 2.5
 score_scale = 192.0 ** (-0.5)
-STOPS = (2, 5, 10, 13)
+STOPS = (1, 2, 4, 6)
 MESH = pl.DeviceIdType.MESH
 F32 = jnp.float32
 BF16 = jnp.bfloat16
@@ -69,6 +69,7 @@
     key_recv,
     q_buf,
     kv_buf,
+    rope_in,
     acc,
     peaks,
     masses,
@@ -105,9 +106,9 @@
     tokens, d_loc = hidden.shape
     d_all = d_loc * n_tp
     lat = kv_gain.shape[1]
-    kvc = cache.shape[2]
+    pairs, span_len, kvc = cache.shape[0], cache.shape[2], cache.shape[3]
     tp = lax.axis_index("tp")
-    chained = 1 < n_ep <= 4
+    staged = 1 < n_ep <= 4
     me = lax.axis_index("ep") * n_mb + lax.axis_index("mb")
 
     def tp_id(step):
@@ -126,7 +127,15 @@
         pltpu.make_async_copy(w_down.at[0], wd, load_sem.at[4]),
         pltpu.make_async_copy(w_dkv, wk, load_sem.at[5]),
     ]
-    kv_load = pltpu.make_async_copy(cache, kv_buf.at[:, tp], kv_load_sem)
+    rope = kvc - lat
+    lanes = kv_buf.shape[3]
+    kv_loads = [
+        pltpu.make_async_copy(
+            cache.at[:, i, :, :lat], kv_buf.at[:, tp, :, i * lat : (i + 1) * lat], kv_load_sem.at[i]
+        )
+        for i in range(2)
+    ]
+    kv_loads.append(pltpu.make_async_copy(cache.at[:, :, :, lat:], rope_in, kv_load_sem.at[2]))
     small = [
         pltpu.make_async_copy(src, dst, small_sem.at[i])
         for i, (src, dst) in enumerate(
@@ -144,7 +153,8 @@
     for copy in small[:4]:
         copy.start()
     local[0].start()
-    kv_load.start()
+    for copy in kv_loads:
+        copy.start()
     for copy in small[4:]:
         copy.start()
 
@@ -156,40 +166,43 @@
 
     for step in range(1, n_tp):
         hello(barrier, {"tp": tp_id(step)})
-    if chained:
+    if staged:
         for step in range(1, n_mb):
             hello(barrier, {"mb": lax.rem(mb + step, n_mb)})
-        greeted = n_tp - 1 + n_mb - 1 + n_mb * jnp.minimum(ep, 1)
+        for far in range(1, n_ep):
+
+            @pl.when(ep + far < n_ep)
+            def _():
+                for m in range(n_mb):
+                    hello(barrier, {"ep": ep + far, "mb": m})
+
+        greeted = n_tp - 1 + n_mb - 1 + n_mb * ep
     else:
         for step in range(1, experts):
             hello(barrier, ex_dev(ex_id(step)))
         greeted = n_tp - 1 + experts - 1
-    for copy in small[:4]:
-        copy.wait()
-    gain_all[tp] = moe_gain[...].reshape(1, d_loc)
-    kept = slots[...] < CAP
-    aff = affinity[...]
-    weight = route_scale * aff / jnp.sum(aff, 0, keepdims=True) * kept.astype(F32)
-    target = jnp.where(kept, ids[...] * CAP + slots[...], -1)
-    rows = experts * CAP
-    iota = lax.broadcasted_iota(jnp.int32, (rows, tokens), 0)
-    dispatch = jnp.zeros((rows, tokens), F32)
-    combine = jnp.zeros((rows, tokens), F32)
-    for k in range(ids.shape[0]):
-        match = target[k : k + 1] == iota
-        dispatch = jnp.where(match, 1.0, dispatch)
-        combine = jnp.where(match, weight[k : k + 1], combine)
-    dispatch = dispatch.astype(BF16)
-    combine = combine.T
-    high = combine.astype(BF16)
-    rest = combine - high.astype(F32)
-    mid = rest.astype(BF16)
-    low = (rest - mid.astype(F32)).astype(BF16)
-    combine3 = jnp.concatenate([high, mid, low], 0)
-
-    def pick(block):
-        picked = jnp.dot(dispatch, hid_all[block], preferred_element_type=F32)
-        send[:, block] = picked.reshape(experts, CAP, d_loc).astype(BF16)
+
+    def tp_copy(src, dst, ssem, rsem, step):
+        return pltpu.make_async_remote_copy(
+            src_ref=src,
+            dst_ref=dst,
+            send_sem=ssem,
+            recv_sem=rsem,
+            device_id={"tp": tp_id(step)},
+            device_id_type=MESH,
+        )
+
+    def arrival(dst, rsem):
+        return pltpu.make_async_copy(dst, dst, rsem)
+
+    def cache_copy(t, step):
+        return tp_copy(
+            kv_buf.at[t, tp], kv_buf.at[t, tp], kv_ssem.at[step, t], kv_rsem.at[tp, t], step
+        )
+
+    def feed(t):
+        for step in range(1, n_tp):
+            cache_copy(t, step).start()
 
     def row_copy(peer, block):
         return pltpu.make_async_remote_copy(
@@ -215,39 +228,10 @@
         for far in range(1, n_ep):
             pl.when(ep >= far)(functools.partial(ship_to, ep - far, block))
             pl.when(ep + far < n_ep)(functools.partial(ship_to, ep + far, block))
+    small[3].wait()
+    gain_all[tp] = moe_gain[...].reshape(1, d_loc)
     local[0].wait()
-    pick(tp)
-    kv_load.wait()
-    for copy in local[1:]:
-        copy.start()
     pl.semaphore_wait(barrier, greeted)
-    if chained:
-
-        @pl.when(ep + 1 < n_ep)
-        def _():
-            for m in range(n_mb):
-                hello(barrier, {"ep": ep + 1, "mb": m})
-
-        for far in range(1, n_ep):
-
-            @pl.when(ep >= far)
-            def _():
-                for m in range(n_mb):
-                    hello(near_sem.at[far], {"ep": ep - far, "mb": m})
-
-
-    def tp_copy(src, dst, ssem, rsem, step):
-        return pltpu.make_async_remote_copy(
-            src_ref=src,
-            dst_ref=dst,
-            send_sem=ssem,
-            recv_sem=rsem,
-            device_id={"tp": tp_id(step)},
-            device_id_type=MESH,
-        )
-
-    def arrival(dst, rsem):
-        return pltpu.make_async_copy(dst, dst, rsem)
     sends = []
     for step in range(1, n_tp):
         for src, dst, ssem, rsem in (
@@ -257,30 +241,63 @@
             copy = tp_copy(src, dst.at[tp], ssem.at[step], rsem.at[tp], step)
             copy.start()
             sends.append(copy)
-
-    def cache_copy(t, step):
-        return tp_copy(
-            kv_buf.at[t, tp], kv_buf.at[t, tp], kv_ssem.at[step, t], kv_rsem.at[tp, t], step
-        )
-
-    def feed(t):
-        for step in range(1, n_tp):
-            cache_copy(t, step).start()
-
-    for t in range(AHEAD):
-        feed(t)
-    if chained:
+    if staged:
+        for far in range(1, n_ep):
+
+            @pl.when(ep >= far)
+            def _():
+                for m in range(n_mb):
+                    hello(near_sem.at[far], {"ep": ep - far, "mb": m})
+
+    for copy in small[:3]:
+        copy.wait()
+    kept = slots[...] < CAP
+    target = jnp.where(kept, ids[...] * CAP + slots[...], -1)
+    rows = experts * CAP
+    iota = lax.broadcasted_iota(jnp.int32, (rows, tokens), 0)
+    dispatch = jnp.zeros((rows, tokens), F32)
+    for k in range(ids.shape[0]):
+        dispatch = jnp.where(target[k : k + 1] == iota, 1.0, dispatch)
+    dispatch = dispatch.astype(BF16)
+
+    def pick(block):
+        picked = jnp.dot(dispatch, hid_all[block], preferred_element_type=F32)
+        send[:, block] = picked.reshape(experts, CAP, d_loc).astype(BF16)
+
+    pick(tp)
+    if staged:
         ship_near(tp)
         for far in range(1, n_ep):
             pl.when(ep >= far)(functools.partial(ship_to, ep - far, tp))
+    else:
+        ship(tp)
+    for copy in kv_loads:
+        copy.wait()
+    kv_buf[:, tp, :, 2 * lat : 2 * lat + 2 * rope] = jnp.concatenate(
+        [rope_in[:, 0], rope_in[:, 1]], -1
+    )
+    for t in range(AHEAD):
+        feed(t)
+    for copy in local[1:]:
+        copy.start()
+    aff = affinity[...]
+    weight = route_scale * aff / jnp.sum(aff, 0, keepdims=True) * kept.astype(F32)
+    combine = jnp.zeros((rows, tokens), F32)
+    for k in range(ids.shape[0]):
+        combine = jnp.where(target[k : k + 1] == iota, weight[k : k + 1], combine)
+    combine = combine.T
+    high = combine.astype(BF16)
+    rest = combine - high.astype(F32)
+    mid = rest.astype(BF16)
+    low = (rest - mid.astype(F32)).astype(BF16)
+    combine3 = jnp.concatenate([high, mid, low], 0)
+    if staged:
         for far in range(1, n_ep):
 
             @pl.when(ep + far < n_ep)
             def _():
                 pl.semaphore_wait(near_sem.at[far], n_mb)
                 ship_to(ep + far, tp)
-    else:
-        ship(tp)
     for step in range(1, n_tp):
         arrival(hid_all.at[tp_id(step)], hid_rsem.at[tp_id(step)]).wait()
         arrival(gain_all.at[tp_id(step)], gain_rsem.at[tp_id(step)]).wait()
@@ -290,40 +307,48 @@
 
     local[1].wait()
     heads = queries.shape[1]
-    span_len = cache.shape[1]
     total_len = n_tp * span_len
 
     def attend(first, last):
-        def body(t, carry):
+        def body(p, carry):
             for step in range(1, n_tp):
-                arrival(kv_buf.at[t, tp_id(step)], kv_rsem.at[tp_id(step), t]).wait()
-
-            @pl.when(t + AHEAD < tokens)
+                arrival(kv_buf.at[p, tp_id(step)], kv_rsem.at[tp_id(step), p]).wait()
+
+            @pl.when(p + AHEAD < pairs)
             def _():
-                feed(t + AHEAD)
-
-            block = kv_buf[t].reshape(total_len, kvc)
-            scores = (
-                lax.dot_general(
-                    q_buf[t], block, (((1,), (1,)), ((), ())), preferred_element_type=F32
+                feed(p + AHEAD)
+
+            ropes = kv_buf[p, :, :, 2 * lat :].reshape(total_len, lanes - 2 * lat)
+            gap = jnp.zeros((heads, rope), BF16)
+            turned = [q_buf[2 * p][:, lat:], gap, gap, q_buf[2 * p + 1][:, lat:]]
+            turned = jnp.concatenate(
+                [jnp.concatenate(turned[:2], 1), jnp.concatenate(turned[2:], 1)], 0
+            )
+            turned = lax.dot_general(
+                turned, ropes, (((1,), (1,)), ((), ())), preferred_element_type=F32
+            )
+            for i in range(2):
+                t = 2 * p + i
+                block = kv_buf[p, :, :, i * lat : (i + 1) * lat].reshape(total_len, lat)
+                scores = lax.dot_general(
+                    q_buf[t][:, :lat], block, (((1,), (1,)), ((), ())), preferred_element_type=F32
                 )
-                * score_scale
-            )
-            live = lax.broadcasted_iota(jnp.int32, (heads, total_len), 1) < lengths[t]
-            scores = jnp.where(live, scores, -1e30)
-            peak = jnp.max(scores, -1, keepdims=True)
-            prob = jnp.where(live, jnp.exp(scores - peak), 0.0)
-            mass = jnp.sum(prob, -1, keepdims=True)
-            acc[t] = jnp.dot(prob.astype(BF16), block[:, :lat], preferred_element_type=F32)
-            peaks[t] = jnp.broadcast_to(peak, (heads, 128))
-            masses[t] = jnp.broadcast_to(mass, (heads, 128))
+                scores = (scores + turned[i * heads : (i + 1) * heads]) * score_scale
+                live = lax.broadcasted_iota(jnp.int32, (heads, total_len), 1) < lengths[t]
+                scores = jnp.where(live, scores, -1e30)
+                peak = jnp.max(scores, -1, keepdims=True)
+                prob = jnp.where(live, jnp.exp(scores - peak), 0.0)
+                mass = jnp.sum(prob, -1, keepdims=True)
+                acc[t] = jnp.dot(prob.astype(BF16), block, preferred_element_type=F32)
+                peaks[t] = jnp.broadcast_to(peak, (heads, 128))
+                masses[t] = jnp.broadcast_to(mass, (heads, 128))
             return carry
 
         lax.fori_loop(first, last, body, 0)
 
     for copy in small[4:]:
         copy.wait()
-    stops = [tokens * n // 16 for n in STOPS]
+    stops = [pairs * n // 8 for n in STOPS]
     attend(0, stops[0])
     local[2].wait()
     local[3].wait()
@@ -435,7 +460,7 @@
         copy.start()
         sends.append(copy)
     key_recv[tp] = key_send[...]
-    attend(stops[3], tokens)
+    attend(stops[3], pairs)
     half = (kvc - lat) // 2
     lane = lax.broadcasted_iota(jnp.int32, (tokens, 2 * half), 1)
     pair = jnp.where(lane < half, lane, lane - half).astype(F32)
@@ -460,27 +485,27 @@
         * lax.rsqrt(jnp.mean(latent * latent, -1, keepdims=True) + epsilon)
         * kv_gain[...]
     )
-    rope = down[:, lat:kvc]
-    swapped = jnp.concatenate([rope[:, half:], rope[:, :half]], 1)
-    rope = rope * cos_table + swapped * sin_table
+    turn = down[:, lat:kvc]
+    swapped = jnp.concatenate([turn[:, half:], turn[:, :half]], 1)
+    turn = turn * cos_table + swapped * sin_table
     keys[:, :lat] = latent.astype(BF16)
-    keys[:, lat:kvc] = rope.astype(BF16)
-    pairs = tokens * heads
+    keys[:, lat:kvc] = turn.astype(BF16)
+    rows_all = tokens * heads
     own = lax.dot_general(
-        q_buf[...].reshape(pairs, kvc),
+        q_buf[...].reshape(rows_all, kvc),
         keys[...],
         (((1,), (1,)), ((), ())),
         preferred_element_type=F32,
     )
-    owner = lax.broadcasted_iota(jnp.int32, (pairs, tokens), 0) // heads
-    mine = owner == lax.broadcasted_iota(jnp.int32, (pairs, tokens), 1)
+    owner = lax.broadcasted_iota(jnp.int32, (rows_all, tokens), 0) // heads
+    mine = owner == lax.broadcasted_iota(jnp.int32, (rows_all, tokens), 1)
     own = jnp.sum(jnp.where(mine, own, 0.0), -1, keepdims=True) * score_scale
-    own = jnp.broadcast_to(own, (pairs, 128))
-    peak = peaks[...].reshape(pairs, 128)
+    own = jnp.broadcast_to(own, (rows_all, 128))
+    peak = peaks[...].reshape(rows_all, 128)
     top = jnp.maximum(peak, own)
     factor = jnp.exp(peak - top)
     own_prob = jnp.exp(own - top)
-    inverse = 1.0 / (masses[...].reshape(pairs, 128) * factor + own_prob)
+    inverse = 1.0 / (masses[...].reshape(rows_all, 128) * factor + own_prob)
     old_part[...] = (factor * inverse).reshape(tokens, heads, 128)
     own_part[...] = (own_prob.astype(BF16).astype(F32) * inverse).reshape(tokens, heads, 128)
     for t in range(tokens):
@@ -500,7 +525,7 @@
             cache_copy(t, step).wait_send()
         return carry
 
-    lax.fori_loop(0, tokens, drain, 0)
+    lax.fori_loop(0, pairs, drain, 0)
 
 
 def solution(mesh):
@@ -559,7 +584,8 @@
                 pltpu.VMEM((tokens, wide), BF16),
                 pltpu.VMEM((n_tp, tokens, wide), BF16),
                 pltpu.VMEM((tokens, heads, kvc), BF16),
-                pltpu.VMEM((tokens, n_tp, span, kvc), BF16),
+                pltpu.VMEM((tokens // 2, n_tp, span, up(2 * kvc, 128)), BF16),
+                pltpu.VMEM((tokens // 2, 2, span, kvc - lat), BF16),
                 pltpu.VMEM((tokens, heads, lat), F32),
                 pltpu.VMEM((tokens, heads, 128), F32),
                 pltpu.VMEM((tokens, heads, 128), F32),
@@ -576,13 +602,13 @@
                 dma((7,)),
                 pltpu.SemaphoreType.REGULAR((n_ep,)),
                 dma((6,)),
-                dma,
-                dma((n_tp,)),
-                dma((n_tp,)),
-                dma((n_tp,)),
-                dma((n_tp,)),
-                dma((n_tp, tokens)),
-                dma((n_tp, tokens)),
+                dma((3,)),
+                dma((n_tp,)),
+                dma((n_tp,)),
+                dma((n_tp,)),
+                dma((n_tp,)),
+                dma((n_tp, tokens // 2)),
+                dma((n_tp, tokens // 2)),
                 dma((experts, n_tp)),
                 dma((experts, n_tp)),
                 dma((experts, max(2, n_tp))),
@@ -608,7 +634,7 @@
             w_dkv.T,
             kv_gain[None],
             queries,
-            cache,
+            cache.reshape(tokens // 2, 2, span, kvc),
             lengths,
         )
 

time: 42.3 us -> 38.1 us (0.901)
  Pallas kernels: 40.1 us -> 35.9 us
    pallas_call x1, Pallas kernels: 40.1 us -> 35.9 us  [local(): pl.pallas_call(functools.partial(kernel, n_tp, n_ep, n_mb), out_shape=(pl...]
where the time goes in v4:
time: 38.1 us; the launch traced here: 37.9 us
  Pallas kernels  35.9 us (94%)
  local copies, waits for them, and re-layouts  1.42 us (4%)
  between operations  0.64 us (2%)
    pallas_call x1, Pallas kernels, local(): pl.pallas_call(functools.partial(kernel, n_tp, n_ep, n_mb), out_shape=(pl...  35.9 us
    unnamed x2, local copies, waits for them, and re-layouts  1.42 us

profile of v4, /device:TPU:0, one launch (start us, length us, event | category | flops | bytes accessed | tf_op | source)
XLA Modules:
  0.0 37.9 jit_solution(9196569612103793829)
XLA Ops:
  0.6 35.9 %shard_map.149 = (bf16[16,1792]{1,0:T(8,128)(2,1)S(1)}, bf16[16,32,512]{2,1,0:T(8,128)(2,1)S(1)}) custom-call(bf16[16,1792]{1,0:T(8,128)(2,1)} %hidden.1, f32[1792]{0:T(1024)} %moe_gain_in.1, s32[8,16]{1,0:T(8,128)} %bitcast.8, s32[8,16]{1,0:T(8,128)} %bitcast.9, f32[8,16]{1,0:T(8,128)} %bitcast.10, bf16[1,3584,512]{2,1,0:T(8,128)(2,1)} %w_gate.1, ...), custom_call_target="tpu_custom_call" | custom-call | tf_op jit(solution)/shard_map/pallas_call | solution.py:562
  36.5 0.6 %copy.18 = bf16[16,1792]{1,0:T(8,128)(2,1)} copy(bf16[16,1792]{1,0:T(8,128)(2,1)S(1)} %get-tuple-element.2) | data formatting | bytes 114688
  37.1 0.8 %copy.19 = bf16[16,32,512]{2,1,0:T(8,128)(2,1)} copy(bf16[16,32,512]{2,1,0:T(8,128)(2,1)S(1)} %get-tuple-element.3) | data formatting | bytes 1048576

commit v5 on v4

--- a/solution.py
+++ b/solution.py
@@ -197,7 +197,7 @@
 
     def cache_copy(t, step):
         return tp_copy(
-            kv_buf.at[t, tp], kv_buf.at[t, tp], kv_ssem.at[step, t], kv_rsem.at[tp, t], step
+            kv_buf.at[t, tp], kv_buf.at[t, tp], kv_ssem.at[0], kv_rsem.at[t], step
         )
 
     def feed(t):
@@ -208,8 +208,8 @@
         return pltpu.make_async_remote_copy(
             src_ref=send.at[peer, block],
             dst_ref=arrived.at[me, block],
-            send_sem=row_ssem.at[peer, block],
-            recv_sem=row_rsem.at[me, block],
+            send_sem=row_ssem.at[0],
+            recv_sem=row_rsem.at[block],
             device_id=ex_dev(peer),
             device_id_type=MESH,
         )
@@ -232,15 +232,12 @@
     gain_all[tp] = moe_gain[...].reshape(1, d_loc)
     local[0].wait()
     pl.semaphore_wait(barrier, greeted)
-    sends = []
     for step in range(1, n_tp):
         for src, dst, ssem, rsem in (
             (hid_all.at[tp], hid_all, hid_ssem, hid_rsem),
             (gain_all.at[tp], gain_all, gain_ssem, gain_rsem),
         ):
-            copy = tp_copy(src, dst.at[tp], ssem.at[step], rsem.at[tp], step)
-            copy.start()
-            sends.append(copy)
+            tp_copy(src, dst.at[tp], ssem.at[0], rsem.at[0], step).start()
     if staged:
         for far in range(1, n_ep):
 
@@ -298,9 +295,8 @@
             def _():
                 pl.semaphore_wait(near_sem.at[far], n_mb)
                 ship_to(ep + far, tp)
-    for step in range(1, n_tp):
-        arrival(hid_all.at[tp_id(step)], hid_rsem.at[tp_id(step)]).wait()
-        arrival(gain_all.at[tp_id(step)], gain_rsem.at[tp_id(step)]).wait()
+    arrival(hid_all.at[pl.ds(0, n_tp - 1)], hid_rsem.at[0]).wait()
+    arrival(gain_all.at[pl.ds(0, n_tp - 1)], gain_rsem.at[0]).wait()
     for turn in range(1, n_tp):
         pick(tp_id(turn))
         ship(tp_id(turn))
@@ -311,8 +307,7 @@
 
     def attend(first, last):
         def body(p, carry):
-            for step in range(1, n_tp):
-                arrival(kv_buf.at[p, tp_id(step)], kv_rsem.at[tp_id(step), p]).wait()
+            arrival(kv_buf.at[p, pl.ds(0, n_tp - 1)], kv_rsem.at[p]).wait()
 
             @pl.when(p + AHEAD < pairs)
             def _():
@@ -359,9 +354,7 @@
         b = tp_id(turn)
         if turn == n_tp - 1:
             attend(stops[0], stops[1])
-        for step in range(1, experts):
-            peer = ex_id(step)
-            arrival(arrived.at[peer, b], row_rsem.at[peer, b]).wait()
+        arrival(arrived.at[pl.ds(0, experts - 1), b], row_rsem.at[b]).wait()
         wide = arrived[:, b].astype(F32).reshape(rows, d_loc)
         square = square + jnp.sum(wide * wide, -1, keepdims=True)
         block = (wide * gain_all[b]).astype(BF16)
@@ -398,28 +391,25 @@
             copy = pltpu.make_async_remote_copy(
                 src_ref=ret_send.at[peer, :, columns(first, size)],
                 dst_ref=ret.at[me, :, columns(first, size)],
-                send_sem=ret_ssem.at[step, h],
-                recv_sem=ret_rsem.at[me, h],
+                send_sem=ret_ssem.at[0],
+                recv_sem=ret_rsem.at[h],
                 device_id=ex_dev(peer),
                 device_id_type=MESH,
             )
             copy.start()
-            sends.append(copy)
     ret[me] = ret_send[me]
 
     def exchange(step):
-        copy = tp_copy(
-            rs_send.at[tp_id(step)], rs_recv.at[tp], rs_ssem.at[step], rs_rsem.at[tp], step
-        )
-        copy.start()
-        sends.append(copy)
+        tp_copy(
+            rs_send.at[tp_id(step)], rs_recv.at[tp], rs_ssem.at[0], rs_rsem.at[0], step
+        ).start()
 
     for h, (first, size) in enumerate(pieces):
         if h < 2:
             attend(stops[h + 1], stops[h + 2])
-        for step in range(1, experts):
-            peer = ex_id(step)
-            arrival(ret.at[peer, :, columns(first, size)], ret_rsem.at[peer, h]).wait()
+        arrival(
+            ret.at[pl.ds(0, experts - 1), :, columns(first, size)], ret_rsem.at[h]
+        ).wait()
         for c in range(0, size, width):
             block = ret[:, :, columns(first + c, width)].astype(F32)
             block = block.reshape(rows, width).astype(BF16)
@@ -438,8 +428,7 @@
             exchange(step)
     rs_recv[tp] = rs_send[tp]
     local[5].wait()
-    for step in range(1, n_tp):
-        arrival(rs_recv.at[tp_id(step)], rs_rsem.at[tp_id(step)]).wait()
+    arrival(rs_recv.at[pl.ds(0, n_tp - 1)], rs_rsem.at[0]).wait()
     moe = rs_recv[0].astype(F32)
     for p in range(1, n_tp):
         moe = moe + rs_recv[p].astype(F32)
@@ -456,9 +445,7 @@
     key_send[:, :kvc] = part.astype(BF16)
     key_send[:, kvc:kvp] = split3(square, tail)
     for step in range(1, n_tp):
-        copy = tp_copy(key_send, key_recv.at[tp], key_ssem.at[step], key_rsem.at[tp], step)
-        copy.start()
-        sends.append(copy)
+        tp_copy(key_send, key_recv.at[tp], key_ssem.at[0], key_rsem.at[0], step).start()
     key_recv[tp] = key_send[...]
     attend(stops[3], pairs)
     half = (kvc - lat) // 2
@@ -472,8 +459,7 @@
     angle = place * freq
     cos_table = jnp.cos(angle)
     sin_table = jnp.where(lane < half, -1.0, 1.0) * jnp.sin(angle)
-    for step in range(1, n_tp):
-        arrival(key_recv.at[tp_id(step)], key_rsem.at[tp_id(step)]).wait()
+    arrival(key_recv.at[pl.ds(0, n_tp - 1)], key_rsem.at[0]).wait()
     total = key_recv[0].astype(F32)
     for p in range(1, n_tp):
         total = total + key_recv[p].astype(F32)
@@ -513,19 +499,27 @@
             value = acc[t, :, c : c + 128] * old_part[t]
             key = keys[t : t + 1, c : c + 128].astype(F32)
             latent_out[t, :, c : c + 128] = (value + own_part[t] * key).astype(BF16)
-    for copy in sends:
-        copy.wait_send()
-
-    for step in range(1, experts):
-        for block in range(n_tp):
-            row_copy(ex_id(step), block).wait_send()
-
-    def drain(t, carry):
-        for step in range(1, n_tp):
-            cache_copy(t, step).wait_send()
-        return carry
-
-    lax.fori_loop(0, pairs, drain, 0)
+    for sent, sem in (
+        (send.at[pl.ds(0, experts - 1)], row_ssem),
+        (ret_send.at[pl.ds(0, experts - 1)], ret_ssem),
+        (hid_all.at[pl.ds(0, n_tp - 1)], hid_ssem),
+        (gain_all.at[pl.ds(0, n_tp - 1)], gain_ssem),
+        (rs_send.at[pl.ds(0, n_tp - 1)], rs_ssem),
+        (key_recv.at[pl.ds(0, n_tp - 1)], key_ssem),
+        (kv_buf.at[:, pl.ds(0, n_tp - 1)], kv_ssem),
+    ):
+        arrival(sent, sem.at[0]).wait()
+
+
+def put_out(hidden_in, latent_in, hidden_out, latent_out, sem):
+    copies = [
+        pltpu.make_async_copy(latent_in, latent_out, sem.at[0]),
+        pltpu.make_async_copy(hidden_in, hidden_out, sem.at[1]),
+    ]
+    for copy in copies:
+        copy.start()
+    for copy in copies:
+        copy.wait()
 
 
 def solution(mesh):
@@ -559,7 +553,7 @@
         any_space = pl.BlockSpec(memory_space=pl.ANY)
         vmem = pl.BlockSpec(memory_space=pltpu.VMEM)
         dma = pltpu.SemaphoreType.DMA
-        return pl.pallas_call(
+        results = pl.pallas_call(
             functools.partial(kernel, n_tp, n_ep, n_mb),
             out_shape=(
                 pltpu.VMEM((tokens, d_loc), BF16),
@@ -603,20 +597,20 @@
                 pltpu.SemaphoreType.REGULAR((n_ep,)),
                 dma((6,)),
                 dma((3,)),
+                dma((1,)),
+                dma((1,)),
+                dma((1,)),
+                dma((1,)),
+                dma((1,)),
+                dma((tokens // 2,)),
+                dma((1,)),
                 dma((n_tp,)),
-                dma((n_tp,)),
-                dma((n_tp,)),
-                dma((n_tp,)),
-                dma((n_tp, tokens // 2)),
-                dma((n_tp, tokens // 2)),
-                dma((experts, n_tp)),
-                dma((experts, n_tp)),
-                dma((experts, max(2, n_tp))),
-                dma((experts, max(2, n_tp))),
-                dma((n_tp,)),
-                dma((n_tp,)),
-                dma((n_tp,)),
-                dma((n_tp,)),
+                dma((1,)),
+                dma((max(2, n_tp),)),
+                dma((1,)),
+                dma((1,)),
+                dma((1,)),
+                dma((1,)),
             ],
             compiler_params=pltpu.CompilerParams(
                 collective_id=0, has_side_effects=True, vmem_limit_bytes=60 * 1024 * 1024
@@ -637,6 +631,16 @@
             cache.reshape(tokens // 2, 2, span, kvc),
             lengths,
         )
+        return pl.pallas_call(
+            put_out,
+            out_shape=(
+                jax.ShapeDtypeStruct((tokens, d_loc), BF16),
+                jax.ShapeDtypeStruct((tokens, heads, lat), BF16),
+            ),
+            in_specs=[vmem, vmem],
+            out_specs=(any_space, any_space),
+            scratch_shapes=[dma((2,))],
+        )(*[pltpu.with_memory_space_constraint(r, pltpu.VMEM) for r in results])
 
     return jax.shard_map(
         local,

time: 38.1 us -> 36.6 us (0.961)
  local copies, waits for them, and re-layouts: 1.42 us -> 0 us
    unnamed x2 -> x0, local copies, waits for them, and re-layouts: 1.42 us -> none
    pallas_call x1, Pallas kernels: 35.9 us -> 35 us  [local(): pl.pallas_call(functools.partial(kernel, n_tp, n_ep, n_mb), out_shape=(pl...]
    pallas_call x0 -> x1, Pallas kernels: none -> 0.81 us  [local(): pl.pallas_call(put_out, out_shape=(jax.ShapeDtypeStruct((tokens, d_loc),...]
where the time goes in v5:
time: 36.6 us; the launch traced here: 36.4 us
  Pallas kernels  35.8 us (98%)
  between operations  0.64 us (2%)
    pallas_call x1, Pallas kernels, local(): pl.pallas_call(functools.partial(kernel, n_tp, n_ep, n_mb), out_shape=(pl...  35 us
    pallas_call x1, Pallas kernels, local(): pl.pallas_call(put_out, out_shape=(jax.ShapeDtypeStruct((tokens, d_loc),...  0.81 us

profile of v5, /device:TPU:0, one launch (start us, length us, event | category | flops | bytes accessed | tf_op | source)
XLA Modules:
  0.0 36.4 jit_solution(3770132586817827467)
XLA Ops:
  0.6 35.0 %shard_map.149 = (bf16[16,1792]{1,0:T(8,128)(2,1)S(1)}, bf16[16,32,512]{2,1,0:T(8,128)(2,1)S(1)}) custom-call(bf16[16,1792]{1,0:T(8,128)(2,1)} %hidden.1, f32[1792]{0:T(1024)} %moe_gain_in.1, s32[8,16]{1,0:T(8,128)} %bitcast.8, s32[8,16]{1,0:T(8,128)} %bitcast.9, f32[8,16]{1,0:T(8,128)} %bitcast.10, bf16[1,3584,512]{2,1,0:T(8,128)(2,1)} %w_gate.1, ...), custom_call_target="tpu_custom_call" | custom-call | tf_op jit(solution)/shard_map/pallas_call | solution.py:556
  35.6 0.8 %shard_map.150 = (bf16[16,1792]{1,0:T(8,128)(2,1)}, bf16[16,32,512]{2,1,0:T(8,128)(2,1)}) custom-call(bf16[16,1792]{1,0:T(8,128)(2,1)S(1)} %get-tuple-element.4.hidden_in, bf16[16,32,512]{2,1,0:T(8,128)(2,1)S(1)} %get-tuple-element.5.latent_in), custom_call_target="tpu_custom_call" | custom-call | tf_op jit(solution)/shard_map/pallas_call | solution.py:634

commit v6 on v5

--- a/solution.py
+++ b/solution.py
@@ -8,11 +8,11 @@
 from jax.sharding import PartitionSpec as P
 
 CAP = 8
-AHEAD = 3
+AHEAD = 4
 epsilon = 1e-06
 route_scale = 2.5
 score_scale = 192.0 ** (-0.5)
-STOPS = (1, 2, 4, 6)
+STOPS = (1, 4, 6, 8)
 MESH = pl.DeviceIdType.MESH
 F32 = jnp.float32
 BF16 = jnp.bfloat16
@@ -67,9 +67,18 @@
     rs_recv,
     key_send,
     key_recv,
-    q_buf,
-    kv_buf,
-    rope_in,
+    q_all,
+    q_rope,
+    k_lat,
+    k_rope,
+    k_pad,
+    o_send,
+    o_recv,
+    stat_send,
+    stat_recv,
+    mid_units,
+    mid_key,
+    gain_row,
     acc,
     peaks,
     masses,
@@ -86,13 +95,18 @@
     small_sem,
     near_sem,
     load_sem,
+    q_sem,
     kv_load_sem,
     hid_ssem,
     hid_rsem,
     gain_ssem,
     gain_rsem,
-    kv_ssem,
-    kv_rsem,
+    q_ssem,
+    q_rsem,
+    o_ssem,
+    o_rsem,
+    stat_ssem,
+    stat_rsem,
     row_ssem,
     row_rsem,
     ret_ssem,
@@ -121,21 +135,23 @@
         return {"ep": index // n_mb, "mb": lax.rem(index, n_mb)}
     local = [
         pltpu.make_async_copy(hidden, hid_all.at[tp], load_sem.at[0]),
-        pltpu.make_async_copy(queries, q_buf, load_sem.at[1]),
         pltpu.make_async_copy(w_gate.at[0], wg, load_sem.at[2]),
         pltpu.make_async_copy(w_up.at[0], wu, load_sem.at[3]),
         pltpu.make_async_copy(w_down.at[0], wd, load_sem.at[4]),
         pltpu.make_async_copy(w_dkv, wk, load_sem.at[5]),
     ]
     rope = kvc - lat
-    lanes = kv_buf.shape[3]
-    kv_loads = [
+    q_loads = [
         pltpu.make_async_copy(
-            cache.at[:, i, :, :lat], kv_buf.at[:, tp, :, i * lat : (i + 1) * lat], kv_load_sem.at[i]
+            queries.at[:, i, :, :lat], q_all.at[:, 0, :, i * lat : (i + 1) * lat], q_sem.at[i]
         )
         for i in range(2)
     ]
-    kv_loads.append(pltpu.make_async_copy(cache.at[:, :, :, lat:], rope_in, kv_load_sem.at[2]))
+    q_loads.append(pltpu.make_async_copy(queries.at[:, :, :, lat:], q_rope, q_sem.at[2]))
+    kv_loads = [
+        pltpu.make_async_copy(cache.at[:, :, :, :lat], k_lat, kv_load_sem.at[0]),
+        pltpu.make_async_copy(cache.at[:, :, :, lat:], k_rope, kv_load_sem.at[1]),
+    ]
     small = [
         pltpu.make_async_copy(src, dst, small_sem.at[i])
         for i, (src, dst) in enumerate(
@@ -153,7 +169,7 @@
     for copy in small[:4]:
         copy.start()
     local[0].start()
-    for copy in kv_loads:
+    for copy in q_loads + kv_loads:
         copy.start()
     for copy in small[4:]:
         copy.start()
@@ -195,14 +211,11 @@
     def arrival(dst, rsem):
         return pltpu.make_async_copy(dst, dst, rsem)
 
-    def cache_copy(t, step):
-        return tp_copy(
-            kv_buf.at[t, tp], kv_buf.at[t, tp], kv_ssem.at[0], kv_rsem.at[t], step
-        )
-
-    def feed(t):
+    def feed(p):
         for step in range(1, n_tp):
-            cache_copy(t, step).start()
+            tp_copy(
+                q_all.at[p, 0], q_all.at[p, n_tp - step], q_ssem.at[0], q_rsem.at[p], step
+            ).start()
 
     def row_copy(peer, block):
         return pltpu.make_async_remote_copy(
@@ -268,15 +281,19 @@
             pl.when(ep >= far)(functools.partial(ship_to, ep - far, tp))
     else:
         ship(tp)
-    for copy in kv_loads:
+    for copy in q_loads:
         copy.wait()
-    kv_buf[:, tp, :, 2 * lat : 2 * lat + 2 * rope] = jnp.concatenate(
-        [rope_in[:, 0], rope_in[:, 1]], -1
-    )
+    q_all[:, 0, :, 2 * lat : 2 * kvc] = jnp.concatenate([q_rope[:, 0], q_rope[:, 1]], -1)
     for t in range(AHEAD):
         feed(t)
     for copy in local[1:]:
         copy.start()
+    for copy in kv_loads:
+        copy.wait()
+    blank = jnp.zeros((pairs, span_len, rope), BF16)
+    k_pad[:, :span_len] = jnp.concatenate([k_rope[:, 0], blank], -1)
+    k_pad[:, span_len:] = jnp.concatenate([blank, k_rope[:, 1]], -1)
+    stat_send[...] = jnp.zeros(stat_send.shape, F32)
     aff = affinity[...]
     weight = route_scale * aff / jnp.sum(aff, 0, keepdims=True) * kept.astype(F32)
     combine = jnp.zeros((rows, tokens), F32)
@@ -301,54 +318,75 @@
         pick(tp_id(turn))
         ship(tp_id(turn))
 
-    local[1].wait()
-    heads = queries.shape[1]
-    total_len = n_tp * span_len
+    heads = queries.shape[2]
+    both = n_tp * heads
+    keys_two = 2 * span_len
+    lane = lax.broadcasted_iota(jnp.int32, (both, keys_two), 1)
+    first_token = lane < span_len
+    stat_lane = lax.broadcasted_iota(jnp.int32, stat_send.shape[1:], 1)
 
     def attend(first, last):
         def body(p, carry):
-            arrival(kv_buf.at[p, pl.ds(0, n_tp - 1)], kv_rsem.at[p]).wait()
+            arrival(q_all.at[p, pl.ds(1, n_tp - 1)], q_rsem.at[p]).wait()
 
             @pl.when(p + AHEAD < pairs)
             def _():
                 feed(p + AHEAD)
 
-            ropes = kv_buf[p, :, :, 2 * lat :].reshape(total_len, lanes - 2 * lat)
-            gap = jnp.zeros((heads, rope), BF16)
-            turned = [q_buf[2 * p][:, lat:], gap, gap, q_buf[2 * p + 1][:, lat:]]
-            turned = jnp.concatenate(
-                [jnp.concatenate(turned[:2], 1), jnp.concatenate(turned[2:], 1)], 0
+            q = q_all[p].reshape(both, q_all.shape[3])
+            block = k_lat[p].reshape(keys_two, lat)
+            crossed = lax.dot_general(
+                jnp.concatenate([q[:, :lat], q[:, lat : 2 * lat]], 0),
+                block,
+                (((1,), (1,)), ((), ())),
+                preferred_element_type=F32,
             )
             turned = lax.dot_general(
-                turned, ropes, (((1,), (1,)), ((), ())), preferred_element_type=F32
+                q[:, 2 * lat :], k_pad[p], (((1,), (1,)), ((), ())), preferred_element_type=F32
+            )
+            scores = (jnp.where(first_token, crossed[:both], crossed[both:]) + turned) * score_scale
+            done = tp * span_len
+            stop = jnp.where(first_token, lengths[2 * p] - done, lengths[2 * p + 1] - done + span_len)
+            live = lane < stop
+            scores = jnp.where(live, scores, -1e30)
+            mine = [first_token, jnp.logical_not(first_token)]
+            tops = [
+                jnp.max(jnp.where(m, scores, -1e30), -1, keepdims=True).astype(BF16).astype(F32)
+                for m in mine
+            ]
+            prob = jnp.where(live, jnp.exp(scores - jnp.where(first_token, tops[0], tops[1])), 0.0)
+            parts = [jnp.where(m, prob, 0.0) for m in mine]
+            sums = [jnp.sum(part, -1, keepdims=True) for part in parts]
+            out = jnp.dot(
+                jnp.concatenate(parts, 0).astype(BF16), block, preferred_element_type=F32
             )
             for i in range(2):
-                t = 2 * p + i
-                block = kv_buf[p, :, :, i * lat : (i + 1) * lat].reshape(total_len, lat)
-                scores = lax.dot_general(
-                    q_buf[t][:, :lat], block, (((1,), (1,)), ((), ())), preferred_element_type=F32
-                )
-                scores = (scores + turned[i * heads : (i + 1) * heads]) * score_scale
-                live = lax.broadcasted_iota(jnp.int32, (heads, total_len), 1) < lengths[t]
-                scores = jnp.where(live, scores, -1e30)
-                peak = jnp.max(scores, -1, keepdims=True)
-                prob = jnp.where(live, jnp.exp(scores - peak), 0.0)
-                mass = jnp.sum(prob, -1, keepdims=True)
-                acc[t] = jnp.dot(prob.astype(BF16), block, preferred_element_type=F32)
-                peaks[t] = jnp.broadcast_to(peak, (heads, 128))
-                masses[t] = jnp.broadcast_to(mass, (heads, 128))
+                acc[2 * p + i] = out[i * both : i * both + heads]
+                peaks[2 * p + i] = jnp.broadcast_to(tops[i][:heads], (heads, 128))
+                masses[2 * p + i] = jnp.broadcast_to(sums[i][:heads], (heads, 128))
+            for step in range(1, n_tp):
+                stat = stat_send[step]
+                for i in range(2):
+                    start = step * heads
+                    o_send[step, p, i] = out[i * both + start : i * both + start + heads].astype(BF16)
+                    base = 2 * (2 * p + i)
+                    stat = jnp.where(stat_lane == base, tops[i][start : start + heads], stat)
+                    stat = jnp.where(stat_lane == base + 1, sums[i][start : start + heads], stat)
+                stat_send[step] = stat
+                tp_copy(
+                    o_send.at[step, p], o_recv.at[n_tp - step, p], o_ssem.at[0], o_rsem.at[0], step
+                ).start()
             return carry
 
         lax.fori_loop(first, last, body, 0)
 
     for copy in small[4:]:
         copy.wait()
+    gain_row[...] = attn_gain[...].reshape(1, d_loc)
     stops = [pairs * n // 8 for n in STOPS]
     attend(0, stops[0])
+    local[1].wait()
     local[2].wait()
-    local[3].wait()
-    gate = jnp.zeros((rows, wg.shape[1]), F32)
-    upper = jnp.zeros((rows, wg.shape[1]), F32)
     square = jnp.zeros((rows, 1), F32)
     for turn in range(n_tp):
         b = tp_id(turn)
@@ -359,20 +397,25 @@
         square = square + jnp.sum(wide * wide, -1, keepdims=True)
         block = (wide * gain_all[b]).astype(BF16)
         deep = pl.ds(pl.multiple_of(b * d_loc, d_loc & -d_loc), d_loc)
-        gate = gate + jnp.dot(block, wg[deep], preferred_element_type=F32)
-        upper = upper + jnp.dot(block, wu[deep], preferred_element_type=F32)
+        gate = jnp.dot(block, wg[deep], preferred_element_type=F32)
+        upper = jnp.dot(block, wu[deep], preferred_element_type=F32)
+        if turn > 0:
+            gate = gate + mid_units[0]
+            upper = upper + mid_units[1]
+        if turn < n_tp - 1:
+            mid_units[0] = gate
+            mid_units[1] = upper
     scale = lax.rsqrt(square / d_all + epsilon)
     gate = gate * scale
     upper = upper * scale
     units = (gate / (1.0 + jnp.exp(-gate)) * upper).astype(BF16)
-    local[4].wait()
+    local[3].wait()
     width = 512 if d_all % 512 == 0 else 128
     aligned = d_loc % 128 == 0
     if aligned:
         width = next(w for w in (896, 512, 384, 256, 128) if d_loc % w == 0)
-        pieces = [
-            (pl.multiple_of(tp_id(turn) * d_loc, 128), d_loc) for turn in (*range(1, n_tp), 0)
-        ]
+        pieces = [(tp_id(turn) * d_loc, d_loc) for turn in range(1, n_tp)]
+        pieces += [(tp * d_loc + c, width) for c in range(0, d_loc, width)]
     else:
         middle = d_all // width // 2 * width
         pieces = [(0, middle), (middle, d_all - middle)]
@@ -386,71 +429,114 @@
             ret_send[:, :, columns(first + c, width)] = part.reshape(
                 experts, CAP, width
             ).astype(BF16)
-        for step in range(1, experts):
-            peer = ex_id(step)
-            copy = pltpu.make_async_remote_copy(
-                src_ref=ret_send.at[peer, :, columns(first, size)],
-                dst_ref=ret.at[me, :, columns(first, size)],
-                send_sem=ret_ssem.at[0],
-                recv_sem=ret_rsem.at[h],
-                device_id=ex_dev(peer),
-                device_id_type=MESH,
-            )
-            copy.start()
+            for step in range(1, experts):
+                peer = ex_id(step)
+                pltpu.make_async_remote_copy(
+                    src_ref=ret_send.at[peer, :, columns(first + c, width)],
+                    dst_ref=ret.at[me, :, columns(first + c, width)],
+                    send_sem=ret_ssem.at[0],
+                    recv_sem=ret_rsem.at[h],
+                    device_id=ex_dev(peer),
+                    device_id_type=MESH,
+                ).start()
     ret[me] = ret_send[me]
 
     def exchange(step):
         tp_copy(
-            rs_send.at[tp_id(step)], rs_recv.at[tp], rs_ssem.at[0], rs_rsem.at[0], step
+            rs_send.at[step], rs_recv.at[n_tp - step], rs_ssem.at[0], rs_rsem.at[0], step
         ).start()
 
-    for h, (first, size) in enumerate(pieces):
-        if h < 2:
-            attend(stops[h + 1], stops[h + 2])
+    def gather(h):
+        first, size = pieces[h]
         arrival(
             ret.at[pl.ds(0, experts - 1), :, columns(first, size)], ret_rsem.at[h]
         ).wait()
-        for c in range(0, size, width):
-            block = ret[:, :, columns(first + c, width)].astype(F32)
-            block = block.reshape(rows, width).astype(BF16)
-            part = jnp.dot(combine3, block, preferred_element_type=F32)
-            part = part[:tokens] + (part[tokens : 2 * tokens] + part[2 * tokens : 3 * tokens])
-            if aligned:
-                rs_send[tp_id(h + 1), :, c : c + width] = part.astype(BF16)
-            else:
-                tsum[:, columns(first + c, width)] = part
-        if aligned and h < n_tp - 1:
-            exchange(h + 1)
-    if not aligned:
+
+    def mixed(start):
+        block = ret[:, :, columns(start, width)].astype(F32)
+        block = block.reshape(rows, width).astype(BF16)
+        part = jnp.dot(combine3, block, preferred_element_type=F32)
+        return part[:tokens] + (part[tokens : 2 * tokens] + part[2 * tokens : 3 * tokens])
+
+    def send_stats():
+        for step in range(1, n_tp):
+            tp_copy(
+                stat_send.at[step],
+                stat_recv.at[n_tp - step],
+                stat_ssem.at[0],
+                stat_rsem.at[0],
+                step,
+            ).start()
+
+    def renew(start, size, moe):
+        span = pl.ds(start, size)
+        fresh = (hid_all[tp, :, span].astype(F32) + moe).astype(BF16)
+        next_out[:, span] = fresh
+        fresh = fresh.astype(F32)
+        scaled = (fresh * gain_row[...][:, start : start + size]).astype(BF16)
+        part = lax.dot_general(
+            scaled, wk[:, span], (((1,), (1,)), ((), ())), preferred_element_type=F32
+        )
+        return jnp.sum(fresh * fresh, -1, keepdims=True), part
+
+    def others(start, size):
+        total = rs_recv[1, :, pl.ds(start, size)].astype(F32)
+        for step in range(2, n_tp):
+            total = total + rs_recv[step, :, pl.ds(start, size)].astype(F32)
+        return total
+    attend(stops[1], stops[2])
+    if aligned:
+        for turn in range(1, n_tp):
+            gather(turn - 1)
+            for c in range(0, d_loc, width):
+                rs_send[turn, :, c : c + width] = mixed(pieces[turn - 1][0] + c).astype(BF16)
+            exchange(turn)
+        attend(stops[2], stops[3])
+        if stops[3] == pairs:
+            send_stats()
+        local[4].wait()
+        square = jnp.zeros((tokens, 1), F32)
+        for i, c in enumerate(range(0, d_loc, width)):
+            gather(n_tp - 1 + i)
+            part = mixed(tp * d_loc + c)
+            if i == 0:
+                arrival(rs_recv.at[pl.ds(1, n_tp - 1)], rs_rsem.at[0]).wait()
+            more, part = renew(c, width, part + others(c, width))
+            square = square + more
+            if i > 0:
+                part = part + mid_key[...]
+            if c + width < d_loc:
+                mid_key[...] = part
+    else:
+        for h in range(2):
+            gather(h)
+            first, size = pieces[h]
+            for c in range(0, size, width):
+                tsum[:, columns(first + c, width)] = mixed(first + c)
+            if h == 0:
+                attend(stops[2], stops[3])
         for p in range(n_tp):
-            rs_send[p] = tsum[:, p * d_loc : (p + 1) * d_loc].astype(BF16)
+            rs_send[lax.rem(p - tp + n_tp, n_tp)] = tsum[:, p * d_loc : (p + 1) * d_loc].astype(BF16)
         for step in range(1, n_tp):
             exchange(step)
-    rs_recv[tp] = rs_send[tp]
-    local[5].wait()
-    arrival(rs_recv.at[pl.ds(0, n_tp - 1)], rs_rsem.at[0]).wait()
-    moe = rs_recv[0].astype(F32)
-    for p in range(1, n_tp):
-        moe = moe + rs_recv[p].astype(F32)
-    next_hidden = (hid_all[tp].astype(F32) + moe).astype(BF16)
-    next_out[...] = next_hidden
-    next_wide = next_hidden.astype(F32)
-    square = jnp.sum(next_wide * next_wide, -1, keepdims=True)
-    scaled = (next_wide * attn_gain[...].reshape(1, d_loc)).astype(BF16)
+        if stops[3] == pairs:
+            send_stats()
+        local[4].wait()
+        arrival(rs_recv.at[pl.ds(1, n_tp - 1)], rs_rsem.at[0]).wait()
+        square, part = renew(0, d_loc, rs_send[0].astype(F32) + others(0, d_loc))
     kvp = up(kvc + 3, 128)
     tail = kvp - kvc
-    part = lax.dot_general(
-        scaled, wk[...], (((1,), (1,)), ((), ())), preferred_element_type=F32
-    )
     key_send[:, :kvc] = part.astype(BF16)
     key_send[:, kvc:kvp] = split3(square, tail)
     for step in range(1, n_tp):
         tp_copy(key_send, key_recv.at[tp], key_ssem.at[0], key_rsem.at[0], step).start()
     key_recv[tp] = key_send[...]
-    attend(stops[3], pairs)
+    if stops[3] < pairs:
+        attend(stops[3], pairs)
+        send_stats()
     half = (kvc - lat) // 2
-    lane = lax.broadcasted_iota(jnp.int32, (tokens, 2 * half), 1)
-    pair = jnp.where(lane < half, lane, lane - half).astype(F32)
+    column = lax.broadcasted_iota(jnp.int32, (tokens, 2 * half), 1)
+    pair = jnp.where(column < half, column, column - half).astype(F32)
     freq = jnp.exp(pair * (-9.210340371976184 / half))
     row_id = lax.broadcasted_iota(jnp.int32, (tokens, 2 * half), 0)
     place = jnp.zeros((tokens, 2 * half), F32)
@@ -458,7 +544,23 @@
         place = jnp.where(row_id == t, lengths[t].astype(F32), place)
     angle = place * freq
     cos_table = jnp.cos(angle)
-    sin_table = jnp.where(lane < half, -1.0, 1.0) * jnp.sin(angle)
+    sin_table = jnp.where(column < half, -1.0, 1.0) * jnp.sin(angle)
+    arrival(o_recv.at[pl.ds(1, n_tp - 1)], o_rsem.at[0]).wait()
+    arrival(stat_recv.at[pl.ds(1, n_tp - 1)], stat_rsem.at[0]).wait()
+    for t in range(tokens):
+        for step in range(1, n_tp):
+            stat = stat_recv[step]
+            far_top = jnp.sum(jnp.where(stat_lane == 2 * t, stat, 0.0), -1, keepdims=True)
+            far_mass = jnp.sum(jnp.where(stat_lane == 2 * t + 1, stat, 0.0), -1, keepdims=True)
+            near_top = peaks[t]
+            top = jnp.maximum(near_top, far_top)
+            near_factor = jnp.exp(near_top - top)
+            far_factor = jnp.exp(far_top - top)
+            peaks[t] = top
+            masses[t] = masses[t] * near_factor + far_mass * far_factor
+            for c in range(0, lat, 128):
+                far = o_recv[step, t // 2, t % 2, :, c : c + 128].astype(F32) * far_factor
+                acc[t, :, c : c + 128] = acc[t, :, c : c + 128] * near_factor + far
     arrival(key_recv.at[pl.ds(0, n_tp - 1)], key_rsem.at[0]).wait()
     total = key_recv[0].astype(F32)
     for p in range(1, n_tp):
@@ -475,13 +577,33 @@
     swapped = jnp.concatenate([turn[:, half:], turn[:, :half]], 1)
     turn = turn * cos_table + swapped * sin_table
     keys[:, :lat] = latent.astype(BF16)
-    keys[:, lat:kvc] = turn.astype(BF16)
+    turn = turn.astype(BF16)
+    blank = jnp.zeros((tokens, rope), BF16)
+    keys[:, lat:] = jnp.concatenate([turn, blank, blank, turn], 1)
     rows_all = tokens * heads
-    own = lax.dot_general(
-        q_buf[...].reshape(rows_all, kvc),
-        keys[...],
-        (((1,), (1,)), ((), ())),
-        preferred_element_type=F32,
+    own = jnp.concatenate(
+        [
+            jnp.concatenate(
+                [
+                    lax.dot_general(
+                        q_all[p, 0, :, i * lat : (i + 1) * lat],
+                        keys[:, :lat],
+                        (((1,), (1,)), ((), ())),
+                        preferred_element_type=F32,
+                    )
+                    + lax.dot_general(
+                        q_all[p, 0, :, 2 * lat :],
+                        keys[:, lat + 2 * rope * i : lat + 2 * rope * (i + 1)],
+                        (((1,), (1,)), ((), ())),
+                        preferred_element_type=F32,
+                    )
+                    for i in range(2)
+                ],
+                0,
+            )
+            for p in range(pairs)
+        ],
+        0,
     )
     owner = lax.broadcasted_iota(jnp.int32, (rows_all, tokens), 0) // heads
     mine = owner == lax.broadcasted_iota(jnp.int32, (rows_all, tokens), 1)
@@ -504,9 +626,11 @@
         (ret_send.at[pl.ds(0, experts - 1)], ret_ssem),
         (hid_all.at[pl.ds(0, n_tp - 1)], hid_ssem),
         (gain_all.at[pl.ds(0, n_tp - 1)], gain_ssem),
-        (rs_send.at[pl.ds(0, n_tp - 1)], rs_ssem),
+        (rs_send.at[pl.ds(1, n_tp - 1)], rs_ssem),
         (key_recv.at[pl.ds(0, n_tp - 1)], key_ssem),
-        (kv_buf.at[:, pl.ds(0, n_tp - 1)], kv_ssem),
+        (q_all.at[:, pl.ds(0, n_tp - 1)], q_ssem),
+        (o_send.at[pl.ds(1, n_tp - 1)], o_ssem),
+        (stat_send.at[pl.ds(1, n_tp - 1)], stat_ssem),
     ):
         arrival(sent, sem.at[0]).wait()
 
@@ -547,6 +671,7 @@
         heads, kvc = queries.shape[1:]
         span = cache.shape[1]
         lat = kv_gain.shape[0]
+        pairs = tokens // 2
         hid_dim = w_gate.shape[2]
         top = expert_ids.shape[1]
         wide = up(kvc + 3, 128)
@@ -577,13 +702,22 @@
                 pltpu.VMEM((n_tp, tokens, d_loc), BF16),
                 pltpu.VMEM((tokens, wide), BF16),
                 pltpu.VMEM((n_tp, tokens, wide), BF16),
-                pltpu.VMEM((tokens, heads, kvc), BF16),
-                pltpu.VMEM((tokens // 2, n_tp, span, up(2 * kvc, 128)), BF16),
-                pltpu.VMEM((tokens // 2, 2, span, kvc - lat), BF16),
+                pltpu.VMEM((pairs, n_tp, heads, 2 * kvc), BF16),
+                pltpu.VMEM((pairs, 2, heads, kvc - lat), BF16),
+                pltpu.VMEM((pairs, 2, span, lat), BF16),
+                pltpu.VMEM((pairs, 2, span, kvc - lat), BF16),
+                pltpu.VMEM((pairs, 2 * span, 2 * (kvc - lat)), BF16),
+                pltpu.VMEM((n_tp, pairs, 2, heads, lat), BF16),
+                pltpu.VMEM((n_tp, pairs, 2, heads, lat), BF16),
+                pltpu.VMEM((n_tp, heads, up(2 * tokens, 128)), F32),
+                pltpu.VMEM((n_tp, heads, up(2 * tokens, 128)), F32),
+                pltpu.VMEM((2, experts * CAP, hid_dim), F32),
+                pltpu.VMEM((tokens, kvc), F32),
+                pltpu.VMEM((1, d_loc), F32),
                 pltpu.VMEM((tokens, heads, lat), F32),
                 pltpu.VMEM((tokens, heads, 128), F32),
                 pltpu.VMEM((tokens, heads, 128), F32),
-                pltpu.VMEM((tokens, kvc), BF16),
+                pltpu.VMEM((tokens, lat + 4 * (kvc - lat)), BF16),
                 pltpu.VMEM((tokens, heads, 128), F32),
                 pltpu.VMEM((tokens, heads, 128), F32),
                 pltpu.VMEM((d_loc,), F32),
@@ -597,16 +731,21 @@
                 pltpu.SemaphoreType.REGULAR((n_ep,)),
                 dma((6,)),
                 dma((3,)),
-                dma((1,)),
-                dma((1,)),
-                dma((1,)),
-                dma((1,)),
-                dma((1,)),
-                dma((tokens // 2,)),
+                dma((2,)),
+                dma((1,)),
+                dma((1,)),
+                dma((1,)),
+                dma((1,)),
+                dma((1,)),
+                dma((pairs,)),
+                dma((1,)),
+                dma((1,)),
+                dma((1,)),
+                dma((1,)),
                 dma((1,)),
                 dma((n_tp,)),
                 dma((1,)),
-                dma((max(2, n_tp),)),
+                dma((max(2, n_tp - 1 + up(d_loc, 128) // 128),)),
                 dma((1,)),
                 dma((1,)),
                 dma((1,)),
@@ -627,8 +766,8 @@
             attn_gain,
             w_dkv.T,
             kv_gain[None],
-            queries,
-            cache.reshape(tokens // 2, 2, span, kvc),
+            queries.reshape(pairs, 2, heads, kvc),
+            cache.reshape(pairs, 2, span, kvc),
             lengths,
         )
         return pl.pallas_call(

time: 36.6 us -> 34.9 us (0.954)
  Pallas kernels: 35.8 us -> 34.1 us
    pallas_call x1, Pallas kernels: 35 us -> 33.3 us  [local(): pl.pallas_call(functools.partial(kernel, n_tp, n_ep, n_mb), out_shape=(pl...]
where the time goes in v6:
time: 34.9 us; the launch traced here: 34.7 us
  Pallas kernels  34.1 us (98%)
  between operations  0.64 us (2%)
    pallas_call x1, Pallas kernels, local(): pl.pallas_call(functools.partial(kernel, n_tp, n_ep, n_mb), out_shape=(pl...  33.3 us
    pallas_call x1, Pallas kernels, local(): pl.pallas_call(put_out, out_shape=(jax.ShapeDtypeStruct((tokens, d_loc),...  0.81 us

profile of v6, /device:TPU:0, one launch (start us, length us, event | category | flops | bytes accessed | tf_op | source)
XLA Modules:
  0.0 34.7 jit_solution(12959667294754622151)
XLA Ops:
  0.6 33.3 %shard_map.149 = (bf16[16,1792]{1,0:T(8,128)(2,1)S(1)}, bf16[16,32,512]{2,1,0:T(8,128)(2,1)S(1)}) custom-call(bf16[16,1792]{1,0:T(8,128)(2,1)} %hidden.1, f32[1792]{0:T(1024)} %moe_gain_in.1, s32[8,16]{1,0:T(8,128)} %bitcast.10, s32[8,16]{1,0:T(8,128)} %bitcast.11, f32[8,16]{1,0:T(8,128)} %bitcast.12, bf16[1,3584,512]{2,1,0:T(8,128)(2,1)} %w_gate.1, ...), custom_call_target="tpu_custom_call" | custom-call | tf_op jit(solution)/shard_map/pallas_call | solution.py:681
  33.9 0.8 %shard_map.150 = (bf16[16,1792]{1,0:T(8,128)(2,1)}, bf16[16,32,512]{2,1,0:T(8,128)(2,1)}) custom-call(bf16[16,1792]{1,0:T(8,128)(2,1)S(1)} %get-tuple-element.4.hidden_in, bf16[16,32,512]{2,1,0:T(8,128)(2,1)S(1)} %get-tuple-element.5.latent_in), custom_call_target="tpu_custom_call" | custom-call | tf_op jit(solution)/shard_map/pallas_call | solution.py:773

commit v7 on v6

--- a/solution.py
+++ b/solution.py
@@ -20,6 +20,12 @@
 
 def up(value, step):
     return -(-value // step) * step
+
+
+def piece_width(d_loc, d_all):
+    if d_loc % 128 == 0:
+        return next(w for w in (896, 512, 384, 256, 128) if d_loc % w == 0)
+    return 512 if d_all % 512 == 0 else 128
 
 
 def split3(value, width):
@@ -74,6 +80,7 @@
     k_pad,
     o_send,
     o_recv,
+    stat_all,
     stat_send,
     stat_recv,
     mid_units,
@@ -133,12 +140,21 @@
 
     def ex_dev(index):
         return {"ep": index // n_mb, "mb": lax.rem(index, n_mb)}
+
+    ep, mb = lax.axis_index("ep"), lax.axis_index("mb")
+    barrier = pltpu.get_barrier_semaphore()
+
+    def hello(sem, ids):
+        pl.semaphore_signal(sem, inc=1, device_id=ids, device_id_type=MESH)
+
+    for step in range(1, n_tp):
+        hello(barrier, {"tp": tp_id(step)})
     local = [
         pltpu.make_async_copy(hidden, hid_all.at[tp], load_sem.at[0]),
-        pltpu.make_async_copy(w_gate.at[0], wg, load_sem.at[2]),
-        pltpu.make_async_copy(w_up.at[0], wu, load_sem.at[3]),
-        pltpu.make_async_copy(w_down.at[0], wd, load_sem.at[4]),
-        pltpu.make_async_copy(w_dkv, wk, load_sem.at[5]),
+        pltpu.make_async_copy(w_gate.at[0], wg, load_sem.at[1]),
+        pltpu.make_async_copy(w_up.at[0], wu, load_sem.at[2]),
+        pltpu.make_async_copy(w_down.at[0], wd, load_sem.at[3]),
+        pltpu.make_async_copy(w_dkv, wk, load_sem.at[4]),
     ]
     rope = kvc - lat
     q_loads = [
@@ -166,22 +182,14 @@
             )
         )
     ]
-    for copy in small[:4]:
+    local[0].start()
+    for copy in small[3::-1]:
         copy.start()
-    local[0].start()
     for copy in q_loads + kv_loads:
         copy.start()
     for copy in small[4:]:
         copy.start()
 
-    ep, mb = lax.axis_index("ep"), lax.axis_index("mb")
-    barrier = pltpu.get_barrier_semaphore()
-
-    def hello(sem, ids):
-        pl.semaphore_signal(sem, inc=1, device_id=ids, device_id_type=MESH)
-
-    for step in range(1, n_tp):
-        hello(barrier, {"tp": tp_id(step)})
     if staged:
         for step in range(1, n_mb):
             hello(barrier, {"mb": lax.rem(mb + step, n_mb)})
@@ -293,7 +301,7 @@
     blank = jnp.zeros((pairs, span_len, rope), BF16)
     k_pad[:, :span_len] = jnp.concatenate([k_rope[:, 0], blank], -1)
     k_pad[:, span_len:] = jnp.concatenate([blank, k_rope[:, 1]], -1)
-    stat_send[...] = jnp.zeros(stat_send.shape, F32)
+    stat_all[...] = jnp.zeros(stat_all.shape, F32)
     aff = affinity[...]
     weight = route_scale * aff / jnp.sum(aff, 0, keepdims=True) * kept.astype(F32)
     combine = jnp.zeros((rows, tokens), F32)
@@ -365,14 +373,17 @@
                 peaks[2 * p + i] = jnp.broadcast_to(tops[i][:heads], (heads, 128))
                 masses[2 * p + i] = jnp.broadcast_to(sums[i][:heads], (heads, 128))
             for step in range(1, n_tp):
-                stat = stat_send[step]
+                stat = stat_all[step]
                 for i in range(2):
                     start = step * heads
                     o_send[step, p, i] = out[i * both + start : i * both + start + heads].astype(BF16)
-                    base = 2 * (2 * p + i)
+                    base = 3 * (2 * p + i)
+                    mass = sums[i][start : start + heads]
+                    high = mass.astype(BF16).astype(F32)
                     stat = jnp.where(stat_lane == base, tops[i][start : start + heads], stat)
-                    stat = jnp.where(stat_lane == base + 1, sums[i][start : start + heads], stat)
-                stat_send[step] = stat
+                    stat = jnp.where(stat_lane == base + 1, high, stat)
+                    stat = jnp.where(stat_lane == base + 2, mass - high, stat)
+                stat_all[step] = stat
                 tp_copy(
                     o_send.at[step, p], o_recv.at[n_tp - step, p], o_ssem.at[0], o_rsem.at[0], step
                 ).start()
@@ -410,10 +421,9 @@
     upper = upper * scale
     units = (gate / (1.0 + jnp.exp(-gate)) * upper).astype(BF16)
     local[3].wait()
-    width = 512 if d_all % 512 == 0 else 128
     aligned = d_loc % 128 == 0
+    width = piece_width(d_loc, d_all)
     if aligned:
-        width = next(w for w in (896, 512, 384, 256, 128) if d_loc % w == 0)
         pieces = [(tp_id(turn) * d_loc, d_loc) for turn in range(1, n_tp)]
         pieces += [(tp * d_loc + c, width) for c in range(0, d_loc, width)]
     else:
@@ -459,6 +469,7 @@
         return part[:tokens] + (part[tokens : 2 * tokens] + part[2 * tokens : 3 * tokens])
 
     def send_stats():
+        stat_send[...] = stat_all[...].astype(BF16)
         for step in range(1, n_tp):
             tp_copy(
                 stat_send.at[step],
@@ -549,9 +560,11 @@
     arrival(stat_recv.at[pl.ds(1, n_tp - 1)], stat_rsem.at[0]).wait()
     for t in range(tokens):
         for step in range(1, n_tp):
-            stat = stat_recv[step]
-            far_top = jnp.sum(jnp.where(stat_lane == 2 * t, stat, 0.0), -1, keepdims=True)
-            far_mass = jnp.sum(jnp.where(stat_lane == 2 * t + 1, stat, 0.0), -1, keepdims=True)
+            stat = stat_recv[step].astype(F32)
+            far_top = jnp.sum(jnp.where(stat_lane == 3 * t, stat, 0.0), -1, keepdims=True)
+            far_mass = jnp.where(stat_lane == 3 * t + 1, stat, 0.0)
+            far_mass = far_mass + jnp.where(stat_lane == 3 * t + 2, stat, 0.0)
+            far_mass = jnp.sum(far_mass, -1, keepdims=True)
             near_top = peaks[t]
             top = jnp.maximum(near_top, far_top)
             near_factor = jnp.exp(near_top - top)
@@ -636,10 +649,13 @@
 
 
 def put_out(hidden_in, latent_in, hidden_out, latent_out, sem):
-    copies = [
-        pltpu.make_async_copy(latent_in, latent_out, sem.at[0]),
-        pltpu.make_async_copy(hidden_in, hidden_out, sem.at[1]),
-    ]
+    step = latent_in.shape[0] // 4
+    copies = [pltpu.make_async_copy(hidden_in, hidden_out, sem.at[4])]
+    for i in range(4):
+        part = pl.ds(i * step, step)
+        copies.append(
+            pltpu.make_async_copy(latent_in.at[part], latent_out.at[part], sem.at[i])
+        )
     for copy in copies:
         copy.start()
     for copy in copies:
@@ -675,6 +691,7 @@
         hid_dim = w_gate.shape[2]
         top = expert_ids.shape[1]
         wide = up(kvc + 3, 128)
+        returns = n_tp - 1 + d_loc // piece_width(d_loc, d_all) if d_loc % 128 == 0 else 2
         any_space = pl.BlockSpec(memory_space=pl.ANY)
         vmem = pl.BlockSpec(memory_space=pltpu.VMEM)
         dma = pltpu.SemaphoreType.DMA
@@ -709,8 +726,9 @@
                 pltpu.VMEM((pairs, 2 * span, 2 * (kvc - lat)), BF16),
                 pltpu.VMEM((n_tp, pairs, 2, heads, lat), BF16),
                 pltpu.VMEM((n_tp, pairs, 2, heads, lat), BF16),
-                pltpu.VMEM((n_tp, heads, up(2 * tokens, 128)), F32),
-                pltpu.VMEM((n_tp, heads, up(2 * tokens, 128)), F32),
+                pltpu.VMEM((n_tp, heads, up(3 * tokens, 128)), F32),
+                pltpu.VMEM((n_tp, heads, up(3 * tokens, 128)), BF16),
+                pltpu.VMEM((n_tp, heads, up(3 * tokens, 128)), BF16),
                 pltpu.VMEM((2, experts * CAP, hid_dim), F32),
                 pltpu.VMEM((tokens, kvc), F32),
                 pltpu.VMEM((1, d_loc), F32),
@@ -729,7 +747,7 @@
                 pltpu.SMEM((tokens,), jnp.int32),
                 dma((7,)),
                 pltpu.SemaphoreType.REGULAR((n_ep,)),
-                dma((6,)),
+                dma((5,)),
                 dma((3,)),
                 dma((2,)),
                 dma((1,)),
@@ -745,7 +763,7 @@
                 dma((1,)),
                 dma((n_tp,)),
                 dma((1,)),
-                dma((max(2, n_tp - 1 + up(d_loc, 128) // 128),)),
+                dma((returns,)),
                 dma((1,)),
                 dma((1,)),
                 dma((1,)),
@@ -778,7 +796,7 @@
             ),
             in_specs=[vmem, vmem],
             out_specs=(any_space, any_space),
-            scratch_shapes=[dma((2,))],
+            scratch_shapes=[dma((5,))],
         )(*[pltpu.with_memory_space_constraint(r, pltpu.VMEM) for r in results])
 
     return jax.shard_map(

time: 34.9 us -> 34.8 us (level)
  no operation moved by 1% of the time
where the time goes in v7:
time: 34.8 us; the launch traced here: 34.6 us
  Pallas kernels  34 us (98%)
  between operations  0.64 us (2%)
    pallas_call x1, Pallas kernels, local(): pl.pallas_call(functools.partial(kernel, n_tp, n_ep, n_mb), out_shape=(pl...  33.1 us
    pallas_call x1, Pallas kernels, local(): pl.pallas_call(put_out, out_shape=(jax.ShapeDtypeStruct((tokens, d_loc),...  0.85 us

profile of v7, /device:TPU:0, one launch (start us, length us, event | category | flops | bytes accessed | tf_op | source)
XLA Modules:
  0.0 34.6 jit_solution(11359850318503194158)
XLA Ops:
  0.6 33.1 %shard_map.149 = (bf16[16,1792]{1,0:T(8,128)(2,1)S(1)}, bf16[16,32,512]{2,1,0:T(8,128)(2,1)S(1)}) custom-call(bf16[16,1792]{1,0:T(8,128)(2,1)} %hidden.1, f32[1792]{0:T(1024)} %moe_gain_in.1, s32[8,16]{1,0:T(8,128)} %bitcast.10, s32[8,16]{1,0:T(8,128)} %bitcast.11, f32[8,16]{1,0:T(8,128)} %bitcast.12, bf16[1,3584,512]{2,1,0:T(8,128)(2,1)} %w_gate.1, ...), custom_call_target="tpu_custom_call" | custom-call | tf_op jit(solution)/shard_map/pallas_call | solution.py:698
  33.8 0.8 %shard_map.150 = (bf16[16,1792]{1,0:T(8,128)(2,1)}, bf16[16,32,512]{2,1,0:T(8,128)(2,1)}) custom-call(bf16[16,1792]{1,0:T(8,128)(2,1)S(1)} %get-tuple-element.4.hidden_in, bf16[16,32,512]{2,1,0:T(8,128)(2,1)S(1)} %get-tuple-element.5.latent_in), custom_call_target="tpu_custom_call" | custom-call | tf_op jit(solution)/shard_map/pallas_call | solution.py:791

commit v8 on v7

--- a/solution.py
+++ b/solution.py
@@ -578,45 +578,38 @@
     total = key_recv[0].astype(F32)
     for p in range(1, n_tp):
         total = total + key_recv[p].astype(F32)
-    square = jnp.sum(total[:, kvc:], -1, keepdims=True)
-    down = total * lax.rsqrt(square / d_all + epsilon)
-    latent = down[:, :lat]
-    latent = (
-        latent
-        * lax.rsqrt(jnp.mean(latent * latent, -1, keepdims=True) + epsilon)
-        * kv_gain[...]
-    )
-    turn = down[:, lat:kvc]
+    rows_all = tokens * heads
+    turn = total[:, lat:kvc]
     swapped = jnp.concatenate([turn[:, half:], turn[:, :half]], 1)
     turn = turn * cos_table + swapped * sin_table
-    keys[:, :lat] = latent.astype(BF16)
-    turn = turn.astype(BF16)
-    blank = jnp.zeros((tokens, rope), BF16)
-    keys[:, lat:] = jnp.concatenate([turn, blank, blank, turn], 1)
-    rows_all = tokens * heads
+    gained = total[:, :lat] * kv_gain[...]
+    raw = gained.astype(BF16)
+    blank = jnp.zeros((tokens, rope), F32)
+    turns = [jnp.concatenate(p, 1).astype(BF16) for p in ((turn, blank), (blank, turn))]
+
+    def against(columns, key):
+        return lax.dot_general(
+            q_all[:, 0, :, columns].reshape(pairs * heads, -1),
+            key,
+            (((1,), (1,)), ((), ())),
+            preferred_element_type=F32,
+        )
+
+    flat = [against(slice(i * lat, (i + 1) * lat), raw) for i in range(2)]
+    curled = [against(slice(2 * lat, 2 * kvc), turns[i]) for i in range(2)]
+    square = jnp.sum(total[:, kvc:], -1, keepdims=True)
+    spread = jnp.mean(total[:, :lat] * total[:, :lat], -1, keepdims=True)
+    shrink = lax.rsqrt(square / d_all + epsilon)
+    level = shrink * lax.rsqrt(spread * shrink * shrink + epsilon)
+    keys[...] = (gained * level).astype(BF16)
+    eye = lax.broadcasted_iota(jnp.int32, (tokens, tokens), 0) == lax.broadcasted_iota(
+        jnp.int32, (tokens, tokens), 1
+    )
+    level = jnp.sum(jnp.where(eye, level, 0.0), 0, keepdims=True)
+    shrink = jnp.sum(jnp.where(eye, shrink, 0.0), 0, keepdims=True)
+    halves = [flat[i] * level + curled[i] * shrink for i in range(2)]
     own = jnp.concatenate(
-        [
-            jnp.concatenate(
-                [
-                    lax.dot_general(
-                        q_all[p, 0, :, i * lat : (i + 1) * lat],
-                        keys[:, :lat],
-                        (((1,), (1,)), ((), ())),
-                        preferred_element_type=F32,
-                    )
-                    + lax.dot_general(
-                        q_all[p, 0, :, 2 * lat :],
-                        keys[:, lat + 2 * rope * i : lat + 2 * rope * (i + 1)],
-                        (((1,), (1,)), ((), ())),
-                        preferred_element_type=F32,
-                    )
-                    for i in range(2)
-                ],
-                0,
-            )
-            for p in range(pairs)
-        ],
-        0,
+        [halves[i][p * heads : (p + 1) * heads] for p in range(pairs) for i in range(2)], 0
     )
     owner = lax.broadcasted_iota(jnp.int32, (rows_all, tokens), 0) // heads
     mine = owner == lax.broadcasted_iota(jnp.int32, (rows_all, tokens), 1)
@@ -735,7 +728,7 @@
                 pltpu.VMEM((tokens, heads, lat), F32),
                 pltpu.VMEM((tokens, heads, 128), F32),
                 pltpu.VMEM((tokens, heads, 128), F32),
-                pltpu.VMEM((tokens, lat + 4 * (kvc - lat)), BF16),
+                pltpu.VMEM((tokens, lat), BF16),
                 pltpu.VMEM((tokens, heads, 128), F32),
                 pltpu.VMEM((tokens, heads, 128), F32),
                 pltpu.VMEM((d_loc,), F32),

time: 34.8 us -> 34.6 us (level)
  no operation moved by 1% of the time
where the time goes in v8:
time: 34.6 us; the launch traced here: 34.4 us
  Pallas kernels  33.8 us (98%)
  between operations  0.64 us (2%)
    pallas_call x1, Pallas kernels, local(): pl.pallas_call(functools.partial(kernel, n_tp, n_ep, n_mb), out_shape=(pl...  32.9 us
    pallas_call x1, Pallas kernels, local(): pl.pallas_call(put_out, out_shape=(jax.ShapeDtypeStruct((tokens, d_loc),...  0.85 us

profile of v8, /device:TPU:0, one launch (start us, length us, event | category | flops | bytes accessed | tf_op | source)
XLA Modules:
  0.0 34.4 jit_solution(12219484698287033241)
XLA Ops:
  0.6 32.9 %shard_map.149 = (bf16[16,1792]{1,0:T(8,128)(2,1)S(1)}, bf16[16,32,512]{2,1,0:T(8,128)(2,1)S(1)}) custom-call(bf16[16,1792]{1,0:T(8,128)(2,1)} %hidden.1, f32[1792]{0:T(1024)} %moe_gain_in.1, s32[8,16]{1,0:T(8,128)} %bitcast.10, s32[8,16]{1,0:T(8,128)} %bitcast.11, f32[8,16]{1,0:T(8,128)} %bitcast.12, bf16[1,3584,512]{2,1,0:T(8,128)(2,1)} %w_gate.1, ...), custom_call_target="tpu_custom_call" | custom-call | tf_op jit(solution)/shard_map/pallas_call | solution.py:691
  33.6 0.8 %shard_map.150 = (bf16[16,1792]{1,0:T(8,128)(2,1)}, bf16[16,32,512]{2,1,0:T(8,128)(2,1)}) custom-call(bf16[16,1792]{1,0:T(8,128)(2,1)S(1)} %get-tuple-element.4.hidden_in, bf16[16,32,512]{2,1,0:T(8,128)(2,1)S(1)} %get-tuple-element.5.latent_in), custom_call_target="tpu_custom_call" | custom-call | tf_op jit(solution)/shard_map/pallas_call | solution.py:784
